TPU v7x, 32 devices: a whole 2x2x4 slice. The times are simulated.
32 devices in a mesh: sensor: 4 (over y, x), chan: 8 (over z, core).
Axes of the slice: x: 2, y: 2, z: 4, core: 2. Of those that a mesh axis runs over, the one named last changes fastest.
Arguments:
- samples: float32 [2, 128, 512, 128], P(None, 'sensor', 'chan'), may hold values from -6 to 6
- bins: int32 [64], replicated, may hold values from 1 to 511
- offsets: int32 [64], replicated, may hold values from 0 to 15
Outputs:
- gram: float32 [64, 2, 128, 128], P('chan', None, 'sensor')
All inputs are finite; a program needn't handle non-finite values.
Results may differ from a plain program's by a relative error of at most 0.00009.
Values sent between devices are 32-bit elements; how exact they have to be, the bound alone decides.
No kernel may reach another device: no remote copies, remote signals or barrier semaphores. Data moves between devices by JAX's collectives and lax.ppermute only.
A program may use at most 128 MiB of HBM per device.

v0:
```python
import math

import jax
import jax.numpy as jnp
from jax import lax
from jax.sharding import PartitionSpec as P

power_floor = 0.1


def shifted_2(block, axis, distance):
    devices = range(lax.axis_size(axis))
    route = [((i - distance) % len(devices), i) for i in devices]
    return lax.ppermute(block, axis, route)


def dft_table(length):
    indices = jnp.arange(length, dtype=jnp.int32)
    phases = indices[:, None] * indices[None, :] % length
    angles = phases.astype(jnp.float32) * (2.0 * math.pi / length)
    cosine = jnp.cos(angles) / math.sqrt(length)
    sine_part = jnp.sin(angles) / math.sqrt(length)
    upper = jnp.concatenate([cosine, -sine_part], 1)
    bottom = jnp.concatenate([sine_part, cosine], 1)
    return jnp.concatenate([upper, bottom], 0)


def gram_columns(extended, rim_len, bins, offsets, columns, factor):
    column_count = columns.shape[3]
    sensors_here = extended.shape[3]
    chans = extended.shape[0] - rim_len
    length = extended.shape[1] // 2
    flattened = columns.reshape(chans * length, 2 * column_count)

    def one_alpha(cycle_bin, offset):
        start = rim_len - offset
        shifted = lax.dynamic_slice(
            extended,
            (start, cycle_bin, jnp.int32(0), jnp.int32(0)),
            (chans, length, 2, sensors_here),
        )
        return shifted.reshape(chans * length, 2 * sensors_here)

    def one_block(inputs_pair):
        cycle_bins, channel_shifts = inputs_pair
        left_rows = jax.vmap(one_alpha)(cycle_bins, channel_shifts)
        cross = jnp.einsum("akp,kq->apq", left_rows, flattened, precision=lax.Precision.HIGHEST)
        cross = cross.reshape(cross.shape[0], 2, sensors_here, 2, column_count)
        real_sum = cross[:, 0, :, 0] + cross[:, 1, :, 1]
        imag_sum = cross[:, 1, :, 0] - cross[:, 0, :, 1]
        return jnp.stack([real_sum, imag_sum], 1)

    blocks_out = lax.map(one_block, (bins.reshape(-1, 4), offsets.reshape(-1, 4)))
    return blocks_out.reshape(-1, 2, sensors_here, column_count) * factor


def on_device(samples, bins, offsets):
    chan_count = lax.axis_size("chan")
    sensors_here = samples.shape[1]
    blocks_here = samples.shape[2]
    channel_count = samples.shape[3]
    positions = jnp.arange(channel_count, dtype=jnp.float32)
    window = 0.5 - 0.5 * jnp.cos(positions * (2.0 * math.pi / channel_count))
    framed = jnp.concatenate([samples[0] * window, samples[1] * window], 2)
    demodulates = jnp.einsum(
        "sbn,nk->skb", framed, dft_table(channel_count), precision=lax.Precision.HIGHEST
    )
    demodulates = demodulates.reshape(sensors_here, 2, channel_count, blocks_here)
    received = lax.all_to_all(demodulates, "chan", split_axis=2, concat_axis=3, tiled=True)
    length = received.shape[3]
    joined = jnp.concatenate([received[:, 0], received[:, 1]], 2)
    transformed = jnp.einsum(
        "ncf,fg->ncg", joined, dft_table(length), precision=lax.Precision.HIGHEST
    )
    real_part = transformed[..., :length]
    imag_part = transformed[..., length:]
    scaling = 1.0 / jnp.sqrt(real_part * real_part + imag_part * imag_part + power_floor)
    spectra = jnp.stack([real_part * scaling, imag_part * scaling], 1)
    spectra = jnp.transpose(spectra, (2, 3, 1, 0))
    chans = spectra.shape[0]
    length = spectra.shape[1]
    lower_rim = shifted_2(spectra[1:], "chan", 1)
    rim_len = lower_rim.shape[0]
    extended = jnp.concatenate([lower_rim, spectra], 0)
    extended = jnp.concatenate([extended, extended], 1)
    factor = 1.0 / math.sqrt(chans * chan_count * length)
    everyone = lax.all_gather(spectra, "sensor", axis=3, tiled=True)
    partial_value = gram_columns(extended, rim_len, bins, offsets, everyone, factor)
    return lax.psum_scatter(partial_value, "chan", scatter_dimension=0, tiled=True)


def solution(mesh):
    return jax.shard_map(
        on_device,
        mesh=mesh,
        in_specs=(P(None, "sensor", "chan", None), P(), P()),
        out_specs=P("chan", None, "sensor", None),
        check_vma=False,
    )
```

profile of v0, /device:TPU:0, one launch (start us, length us, event | category | flops | bytes accessed | tf_op | source)
XLA Modules:
  0.0 1729.9 jit_solution(3241247846924783304)
XLA Ops:
  42.5 39.9 %all-to-all-done = f32[8,1,65536]{2,1,0:T(1,128)S(1)} async-done(((f32[8,1,65536]{2,1,0:T(1,128)}), f32[8,1,65536]{2,1,0:T(1,128)S(1)}, u32[]{:S(2)}, u32[]{:S(2)}) %all-to-all-start) | async-done | bytes 2097184 | tf_op jit(solution)/shard_map/all_to_all | solution.py:69
  123.6 26.0 %collective-permute-done = f32[15,512,2,32]{1,3,2,0:T(8,128)} collective-permute-done((f32[15,512,2,32]{1,3,2,0:T(8,128)}, f32[15,512,2,32]{1,3,2,0:T(8,128)}, u32[]{:S(2)}, u32[]{:S(2)}) %collective-permute-start) | collective-permute-done | bytes 1966112 | tf_op jit(solution)/shard_map/ppermute | solution.py:14
  156.5 27.6 %copy.31 = f32[31,1024,2,32]{3,2,1,0:T(2,128)} copy(f32[31,1024,2,32]{1,0,3,2:T(8,128)} %maximum_maximum_fusion) | data formatting | bytes 16252928 | tf_op jit(solution)/shard_map/while | solution.py:53
  184.1 21.5 %all-gather.2.cloned.1.call-done = f32[16,512,2,128]{1,0,3,2:T(8,128)} async-done(((f32[16,512,2,32]{1,0,3,2:T(8,128)}), f32[16,512,2,128]{1,0,3,2:T(8,128)}) %all-gather.2.cloned.1.call-update) | async-done | bytes 8388624 | tf_op jit(solution)/shard_map/all_gather | solution.py:87
  205.6 14.6 copy.39
  220.2 1462.8 %while.15 = (s32[]{:T(128)}, f32[16,4,2,32,128]{4,3,1,2,0:T(8,128)}, s32[16,4]{1,0:T(8,128)S(1)}, s32[16,4]{1,0:T(8,128)S(1)}, f32[31,1024,2,32]{3,2,1,0:T(2,128...) while((s32[]{:T(128)}, f32[16,4,2,32,128]{4,3,1,2,0:T(8,128)}, s32[16,4]{1,0:T(8,128)S(1)}, ...), condition=%wide.region_1.2_spmd, body=%wide.region_0.1_spmd.sunk | while | flops 6442516480 | bytes 47056416 | solution.py:53
  220.6 70.8 %while.16 = (s32[]{:T(128)}, f32[31,1024,2,32]{3,2,1,0:T(2,128)}, s32[4,4]{1,0:T(4,128)S(1)}, f32[4,16,512,2,32]{2,1,4,3,0:T(8,128)}, s32[]{:T(128)}) while((s32[]{:T(128)}, f32[31,1024,2,32]{3,2,1,0:T(2,128)}, s32[4,4]{1,0:T(4,128)S(1)}, f32[4,16,512,2,32]{2,1,4,3,0:T(8,128)}, s32[]{:T(128)}) %tuple.55), condition=%wide.while_cond, body=%wide.while_body.sunk | while | flops 2 | bytes 12583545 | solution.py:37
  221.2 8.7 dynamic-slice_bitcast_fusion.2
  256.7 8.7 dynamic-slice_bitcast_fusion.2
  274.4 8.7 dynamic-slice_bitcast_fusion.2
  291.4 9.4 reshape.192
  300.8 10.2 fusion.57
  312.0 70.8 %while.16 = (s32[]{:T(128)}, f32[31,1024,2,32]{3,2,1,0:T(2,128)}, s32[4,4]{1,0:T(4,128)S(1)}, f32[4,16,512,2,32]{2,1,4,3,0:T(8,128)}, s32[]{:T(128)}) while((s32[]{:T(128)}, f32[31,1024,2,32]{3,2,1,0:T(2,128)}, s32[4,4]{1,0:T(4,128)S(1)}, f32[4,16,512,2,32]{2,1,4,3,0:T(8,128)}, s32[]{:T(128)}) %tuple.55), condition=%wide.while_cond, body=%wide.while_body.sunk | while | flops 2 | bytes 12583545 | solution.py:37
  312.7 8.7 dynamic-slice_bitcast_fusion.2
  348.1 8.7 dynamic-slice_bitcast_fusion.2
  365.8 8.7 dynamic-slice_bitcast_fusion.2
  382.8 9.4 reshape.192
  392.2 10.2 fusion.57
  403.5 70.8 %while.16 = (s32[]{:T(128)}, f32[31,1024,2,32]{3,2,1,0:T(2,128)}, s32[4,4]{1,0:T(4,128)S(1)}, f32[4,16,512,2,32]{2,1,4,3,0:T(8,128)}, s32[]{:T(128)}) while((s32[]{:T(128)}, f32[31,1024,2,32]{3,2,1,0:T(2,128)}, s32[4,4]{1,0:T(4,128)S(1)}, f32[4,16,512,2,32]{2,1,4,3,0:T(8,128)}, s32[]{:T(128)}) %tuple.55), condition=%wide.while_cond, body=%wide.while_body.sunk | while | flops 2 | bytes 12583545 | solution.py:37
  404.1 8.7 dynamic-slice_bitcast_fusion.2
  439.5 8.7 dynamic-slice_bitcast_fusion.2
  457.3 8.7 dynamic-slice_bitcast_fusion.2
  474.3 9.4 reshape.192
  483.6 10.2 fusion.57
  494.9 70.8 %while.16 = (s32[]{:T(128)}, f32[31,1024,2,32]{3,2,1,0:T(2,128)}, s32[4,4]{1,0:T(4,128)S(1)}, f32[4,16,512,2,32]{2,1,4,3,0:T(8,128)}, s32[]{:T(128)}) while((s32[]{:T(128)}, f32[31,1024,2,32]{3,2,1,0:T(2,128)}, s32[4,4]{1,0:T(4,128)S(1)}, f32[4,16,512,2,32]{2,1,4,3,0:T(8,128)}, s32[]{:T(128)}) %tuple.55), condition=%wide.while_cond, body=%wide.while_body.sunk | while | flops 2 | bytes 12583545 | solution.py:37
  565.7 9.4 reshape.192
  575.1 10.2 fusion.57
  586.3 70.8 %while.16 = (s32[]{:T(128)}, f32[31,1024,2,32]{3,2,1,0:T(2,128)}, s32[4,4]{1,0:T(4,128)S(1)}, f32[4,16,512,2,32]{2,1,4,3,0:T(8,128)}, s32[]{:T(128)}) while((s32[]{:T(128)}, f32[31,1024,2,32]{3,2,1,0:T(2,128)}, s32[4,4]{1,0:T(4,128)S(1)}, f32[4,16,512,2,32]{2,1,4,3,0:T(8,128)}, s32[]{:T(128)}) %tuple.55), condition=%wide.while_cond, body=%wide.while_body.sunk | while | flops 2 | bytes 12583545 | solution.py:37
  657.1 9.4 reshape.192
  666.5 10.2 fusion.57
  677.7 70.8 %while.16 = (s32[]{:T(128)}, f32[31,1024,2,32]{3,2,1,0:T(2,128)}, s32[4,4]{1,0:T(4,128)S(1)}, f32[4,16,512,2,32]{2,1,4,3,0:T(8,128)}, s32[]{:T(128)}) while((s32[]{:T(128)}, f32[31,1024,2,32]{3,2,1,0:T(2,128)}, s32[4,4]{1,0:T(4,128)S(1)}, f32[4,16,512,2,32]{2,1,4,3,0:T(8,128)}, s32[]{:T(128)}) %tuple.55), condition=%wide.while_cond, body=%wide.while_body.sunk | while | flops 2 | bytes 12583545 | solution.py:37
  748.5 9.4 reshape.192
  757.9 10.2 fusion.57
  769.2 70.8 %while.16 = (s32[]{:T(128)}, f32[31,1024,2,32]{3,2,1,0:T(2,128)}, s32[4,4]{1,0:T(4,128)S(1)}, f32[4,16,512,2,32]{2,1,4,3,0:T(8,128)}, s32[]{:T(128)}) while((s32[]{:T(128)}, f32[31,1024,2,32]{3,2,1,0:T(2,128)}, s32[4,4]{1,0:T(4,128)S(1)}, f32[4,16,512,2,32]{2,1,4,3,0:T(8,128)}, s32[]{:T(128)}) %tuple.55), condition=%wide.while_cond, body=%wide.while_body.sunk | while | flops 2 | bytes 12583545 | solution.py:37
  840.0 9.4 reshape.192
  849.4 10.2 fusion.57
  860.6 70.8 %while.16 = (s32[]{:T(128)}, f32[31,1024,2,32]{3,2,1,0:T(2,128)}, s32[4,4]{1,0:T(4,128)S(1)}, f32[4,16,512,2,32]{2,1,4,3,0:T(8,128)}, s32[]{:T(128)}) while((s32[]{:T(128)}, f32[31,1024,2,32]{3,2,1,0:T(2,128)}, s32[4,4]{1,0:T(4,128)S(1)}, f32[4,16,512,2,32]{2,1,4,3,0:T(8,128)}, s32[]{:T(128)}) %tuple.55), condition=%wide.while_cond, body=%wide.while_body.sunk | while | flops 2 | bytes 12583545 | solution.py:37
  931.4 9.4 reshape.192
  940.8 10.2 fusion.57
  952.0 70.8 %while.16 = (s32[]{:T(128)}, f32[31,1024,2,32]{3,2,1,0:T(2,128)}, s32[4,4]{1,0:T(4,128)S(1)}, f32[4,16,512,2,32]{2,1,4,3,0:T(8,128)}, s32[]{:T(128)}) while((s32[]{:T(128)}, f32[31,1024,2,32]{3,2,1,0:T(2,128)}, s32[4,4]{1,0:T(4,128)S(1)}, f32[4,16,512,2,32]{2,1,4,3,0:T(8,128)}, s32[]{:T(128)}) %tuple.55), condition=%wide.while_cond, body=%wide.while_body.sunk | while | flops 2 | bytes 12583545 | solution.py:37
  1022.8 9.4 reshape.192
  1032.2 10.2 fusion.57
  1043.5 70.8 %while.16 = (s32[]{:T(128)}, f32[31,1024,2,32]{3,2,1,0:T(2,128)}, s32[4,4]{1,0:T(4,128)S(1)}, f32[4,16,512,2,32]{2,1,4,3,0:T(8,128)}, s32[]{:T(128)}) while((s32[]{:T(128)}, f32[31,1024,2,32]{3,2,1,0:T(2,128)}, s32[4,4]{1,0:T(4,128)S(1)}, f32[4,16,512,2,32]{2,1,4,3,0:T(8,128)}, s32[]{:T(128)}) %tuple.55), condition=%wide.while_cond, body=%wide.while_body.sunk | while | flops 2 | bytes 12583545 | solution.py:37
  1114.3 9.4 reshape.192
  1123.6 10.2 fusion.57
  1134.9 70.8 %while.16 = (s32[]{:T(128)}, f32[31,1024,2,32]{3,2,1,0:T(2,128)}, s32[4,4]{1,0:T(4,128)S(1)}, f32[4,16,512,2,32]{2,1,4,3,0:T(8,128)}, s32[]{:T(128)}) while((s32[]{:T(128)}, f32[31,1024,2,32]{3,2,1,0:T(2,128)}, s32[4,4]{1,0:T(4,128)S(1)}, f32[4,16,512,2,32]{2,1,4,3,0:T(8,128)}, s32[]{:T(128)}) %tuple.55), condition=%wide.while_cond, body=%wide.while_body.sunk | while | flops 2 | bytes 12583545 | solution.py:37
  1205.7 9.4 reshape.192
  1215.1 10.2 fusion.57
  1226.3 70.8 %while.16 = (s32[]{:T(128)}, f32[31,1024,2,32]{3,2,1,0:T(2,128)}, s32[4,4]{1,0:T(4,128)S(1)}, f32[4,16,512,2,32]{2,1,4,3,0:T(8,128)}, s32[]{:T(128)}) while((s32[]{:T(128)}, f32[31,1024,2,32]{3,2,1,0:T(2,128)}, s32[4,4]{1,0:T(4,128)S(1)}, f32[4,16,512,2,32]{2,1,4,3,0:T(8,128)}, s32[]{:T(128)}) %tuple.55), condition=%wide.while_cond, body=%wide.while_body.sunk | while | flops 2 | bytes 12583545 | solution.py:37
  1297.1 9.4 reshape.192
  1306.5 10.2 fusion.57
  1317.7 70.8 %while.16 = (s32[]{:T(128)}, f32[31,1024,2,32]{3,2,1,0:T(2,128)}, s32[4,4]{1,0:T(4,128)S(1)}, f32[4,16,512,2,32]{2,1,4,3,0:T(8,128)}, s32[]{:T(128)}) while((s32[]{:T(128)}, f32[31,1024,2,32]{3,2,1,0:T(2,128)}, s32[4,4]{1,0:T(4,128)S(1)}, f32[4,16,512,2,32]{2,1,4,3,0:T(8,128)}, s32[]{:T(128)}) %tuple.55), condition=%wide.while_cond, body=%wide.while_body.sunk | while | flops 2 | bytes 12583545 | solution.py:37
  1388.5 9.4 reshape.192
  1397.9 10.2 fusion.57
  1409.2 70.8 %while.16 = (s32[]{:T(128)}, f32[31,1024,2,32]{3,2,1,0:T(2,128)}, s32[4,4]{1,0:T(4,128)S(1)}, f32[4,16,512,2,32]{2,1,4,3,0:T(8,128)}, s32[]{:T(128)}) while((s32[]{:T(128)}, f32[31,1024,2,32]{3,2,1,0:T(2,128)}, s32[4,4]{1,0:T(4,128)S(1)}, f32[4,16,512,2,32]{2,1,4,3,0:T(8,128)}, s32[]{:T(128)}) %tuple.55), condition=%wide.while_cond, body=%wide.while_body.sunk | while | flops 2 | bytes 12583545 | solution.py:37
  1480.0 9.4 reshape.192
  1489.3 10.2 fusion.57
  1500.6 70.8 %while.16 = (s32[]{:T(128)}, f32[31,1024,2,32]{3,2,1,0:T(2,128)}, s32[4,4]{1,0:T(4,128)S(1)}, f32[4,16,512,2,32]{2,1,4,3,0:T(8,128)}, s32[]{:T(128)}) while((s32[]{:T(128)}, f32[31,1024,2,32]{3,2,1,0:T(2,128)}, s32[4,4]{1,0:T(4,128)S(1)}, f32[4,16,512,2,32]{2,1,4,3,0:T(8,128)}, s32[]{:T(128)}) %tuple.55), condition=%wide.while_cond, body=%wide.while_body.sunk | while | flops 2 | bytes 12583545 | solution.py:37
  1571.4 9.4 reshape.192
  1580.8 10.2 fusion.57
  1592.0 70.8 %while.16 = (s32[]{:T(128)}, f32[31,1024,2,32]{3,2,1,0:T(2,128)}, s32[4,4]{1,0:T(4,128)S(1)}, f32[4,16,512,2,32]{2,1,4,3,0:T(8,128)}, s32[]{:T(128)}) while((s32[]{:T(128)}, f32[31,1024,2,32]{3,2,1,0:T(2,128)}, s32[4,4]{1,0:T(4,128)S(1)}, f32[4,16,512,2,32]{2,1,4,3,0:T(8,128)}, s32[]{:T(128)}) %tuple.55), condition=%wide.while_cond, body=%wide.while_body.sunk | while | flops 2 | bytes 12583545 | solution.py:37
  1662.8 9.4 reshape.192
  1672.2 10.2 fusion.57
  1686.5 36.1 %reduce-scatter.2.cloned.1.call-done = f32[8,2,32,128]{3,2,1,0:T(8,128)} async-done(((f32[64,2,32,128]{3,2,1,0:T(8,128)}), f32[8,2,32,128]{3,2,1,0:T(8,128)}) %reduce-scatter.2.cloned.1.call-update) | async-done | bytes 262160 | tf_op jit(solution)/shard_map/reduce_scatter | solution.py:89
  (518 shorter events, 1158.3 us)
Async XLA Ops:
  27.0 55.4 %all-to-all-start = ((f32[8,1,65536]{2,1,0:T(1,128)}), f32[8,1,65536]{2,1,0:T(1,128)S(1)}, u32[]{:S(2)}, u32[]{:S(2)}) async-start(f32[8,1,65536]{2,1,0:T(1,128)} %reshape.189), calls=%async_computation | async-start | bytes 4194304 | tf_op jit(solution)/shard_map/all_to_all | solution.py:69
  33.3 172.3 %all-gather.2.cloned.1.call-start = ((), (), s32[]{:S(2)}) async-start(), calls=%async_computation.2 | async-start | bytes 10485760 | tf_op jit(solution)/shard_map/all_gather | solution.py:87
  82.4 1.3 copy-start.1
  108.6 1.2 copy-start.2
  108.6 1.5 copy-start.3
  119.0 1.6 copy-start
  119.1 1603.6 %reduce-scatter.2.cloned.1.call-start = ((), (), s32[]{:S(2)}) async-start(), calls=%async_computation.3 | async-start | bytes 2359296 | tf_op jit(solution)/shard_map/reduce_scatter | solution.py:89
  121.0 2.4 copy-start.4
  121.0 2.5 copy-start.5
  123.4 26.2 %collective-permute-start = (f32[15,512,2,32]{1,3,2,0:T(8,128)}, f32[15,512,2,32]{1,3,2,0:T(8,128)}, u32[]{:S(2)}, u32[]{:S(2)}) collective-permute-start(f32[15,512,2,32]{1,3,2,0:T(8,128)} %copy.29), channel_id=1, source_target_pairs={{7,0},{0,1},{1,2},{2,3},{3,4},{4,5},{5,6},{6,7},{15,8},{8,9},{9,10... | collective-permute-start | bytes 5898248 | tf_op jit(solution)/shard_map/ppermute | solution.py:14
Sparse Core Ops, SparseCore 0:
  119.2 86.4 all-gather.1
  1686.6 35.9 reduce-scatter.1
where the time goes:
time: 1760 us; the launch traced here: 1730 us
  local copies, waits for them, and re-layouts  1370 us (78%)
  matrix products  173 us (10%)
  waiting for transfers between devices  124 us (7%)
  other arithmetic  39 us (2%)
    gather x320, local copies, waits for them, and re-layouts  1130 us
    dot_general x16, matrix products, one_block(): jnp.einsum('akp,kq->apq', left_rows, flattened, precision=lax.Precision.H...  163 us
    reshape x16, local copies, waits for them, and re-layouts, one_alpha(): return shifted.reshape(chans * length, 2 * sensors_here)  150 us
    all_to_all x1, waiting for transfers between devices, on_device(): lax.all_to_all(demodulates, 'chan', split_axis=2, concat_axis=3, tiled=True)  39.9 us
    reduce_scatter x1, waiting for transfers between devices, on_device(): lax.psum_scatter(partial_value, 'chan', scatter_dimension=0, tiled=True)  36.1 us
  transfers between devices with their start and end apart: 4, of which 4 were waited for; matrix products, arithmetic and copies ran while one was open for 3% of the time, Pallas kernels for 0%

commit v1 on v0

v1 whole, which is shorter than its diff:
```python
import functools
import math

import jax
import jax.numpy as jnp
import ml_dtypes
import numpy as np
from jax import lax
from jax.experimental import pallas as pl
from jax.experimental.pallas import tpu as pltpu
from jax.sharding import PartitionSpec as P

power_floor = 0.1
f32 = jnp.float32
bf16 = jnp.bfloat16
nt_dims = (((1,), (1,)), ((), ()))
nn_dims = (((1,), (0,)), ((), ()))


def halves(table):
    high = table.astype(np.float32).astype(ml_dtypes.bfloat16)
    low = (table - high.astype(np.float64)).astype(ml_dtypes.bfloat16)
    return high, low


def window_table(length):
    index = np.arange(length)
    angles = 2.0 * math.pi / length * (index[:, None] * index[None, :] % length)
    window = 0.5 - 0.5 * np.cos(2.0 * math.pi / length * index)
    scale = window[None, :] / math.sqrt(length)
    high, low = halves(np.concatenate([np.cos(angles) * scale, np.sin(angles) * scale], 1))
    return high.astype(np.float32), low.astype(np.float32)


def block_table(length, pieces):
    index = np.arange(length)
    angles = 2.0 * math.pi / length * (index[:, None] * index[None, :] % length)
    scale = 1.0 / math.sqrt(length)
    pair = [(t * scale).reshape(pieces, length // pieces, length) for t in (np.cos(angles), np.sin(angles))]
    return halves(np.concatenate(pair, 1).reshape(2 * length, length))


def split(value):
    high = value.astype(bf16)
    return high, (value - high.astype(f32)).astype(bf16)


def dot3(left, right, dims):
    lh, ll = left
    rh, rl = right
    dot = functools.partial(lax.dot_general, dimension_numbers=dims, preferred_element_type=f32)
    return dot(lh, rh) + dot(ll, rh) + dot(lh, rl)


def swap(block, axis, distance):
    size = lax.axis_size(axis)
    return lax.ppermute(block, axis, [(i, i ^ distance) for i in range(size)])


def demod_body(ids, samples, table_high, table_low, *outs):
    channels = table_high.shape[0]
    half = outs[0].shape[0]
    chans = 2 * half
    order = [pl.multiple_of(jnp.bitwise_xor(ids[0], r) * chans, chans) for r in range(channels // chans)]
    table = tuple(
        jnp.concatenate([t[pl.ds(start, chans), :] for start in order], 0).astype(bf16) for t in (table_high, table_low)
    )
    for s in range(samples.shape[1]):
        real = samples[0, s]
        imag = samples[1, s]
        upper = jnp.concatenate([real, imag], 1)
        lower = jnp.concatenate([imag, -real], 1)
        framed = jnp.concatenate([upper, lower], 0)
        result = dot3(table, split(framed), nt_dims)
        for i, out in enumerate(outs):
            out[:, s, :] = result[i * half:(i + 1) * half]


def demodulate(ids, samples, peers):
    _, sensors, blocks, channels = samples.shape
    step = min(8, sensors)
    half = channels // peers // 2
    high, low = window_table(channels)
    whole = pl.BlockSpec((channels, 2 * channels), lambda i, *_: (0, 0))
    return pl.pallas_call(
        demod_body,
        grid_spec=pltpu.PrefetchScalarGridSpec(
            num_scalar_prefetch=1,
            grid=(sensors // step,),
            in_specs=[pl.BlockSpec((2, step, blocks, channels), lambda i, *_: (0, i, 0, 0)), whole, whole],
            out_specs=[pl.BlockSpec((half, step, 2 * blocks), lambda i, *_: (0, i, 0))] * (2 * peers),
        ),
        out_shape=[jax.ShapeDtypeStruct((half, sensors, 2 * blocks), f32)] * (2 * peers),
        name="demod",
    )(ids, samples, jnp.asarray(high), jnp.asarray(low))


def spectra_body(ids, *refs, sources, places):
    received = refs[:sources]
    table_high, table_low = refs[sources:sources + 2]
    outs = refs[sources + 2:-4]
    left_high, left_low, right_high, right_low = refs[-4:]
    half, sensors, width = received[0].shape
    rows = half * sensors
    for r in range(sources):
        block = received[r][...].reshape(rows, width)
        turned = jnp.concatenate([block[:, width // 2:], -block[:, :width // 2]], 1)
        place = slice(r * width, (r + 1) * width)
        left_high[:rows, place], left_low[:rows, place] = split(block)
        left_high[rows:, place], left_low[rows:, place] = split(turned)
        start = pl.multiple_of(jnp.bitwise_xor(ids[0], r) * width, width)
        right_high[place, :] = table_high[pl.ds(start, width), :]
        right_low[place, :] = table_low[pl.ds(start, width), :]
    total = dot3((left_high[...], left_low[...]), (right_high[...], right_low[...]), nn_dims)
    real = total[:rows]
    imag = total[rows:]
    scaling = lax.rsqrt(real * real + imag * imag + power_floor)
    for c, part in enumerate((real * scaling, imag * scaling)):
        part = part.reshape(half, sensors, part.shape[1])
        for out, place in zip(outs, places):
            out[:, c] = part[place]


def whitened(ids, received, pieces):
    sources = len(received)
    half, sensors, width = received[0].shape
    length = sources * width // 2
    rows = 2 * half * sensors
    high, low = block_table(length, sources)
    shapes = [jax.ShapeDtypeStruct((half, 2, sensors, length), f32)]
    places = [slice(0, half)]
    for i in range(pieces):
        shapes.append(jax.ShapeDtypeStruct((half // pieces, 2, sensors, length), f32))
        places.append(slice(i * half // pieces, (i + 1) * half // pieces))
    return pl.pallas_call(
        functools.partial(spectra_body, sources=sources, places=places),
        grid_spec=pltpu.PrefetchScalarGridSpec(
            num_scalar_prefetch=1,
            grid=(1,),
            in_specs=[pl.BlockSpec((half, sensors, width), lambda i, *_: (0, 0, 0))] * sources
            + [pl.BlockSpec((2 * length, length), lambda i, *_: (0, 0))] * 2,
            out_specs=[pl.BlockSpec(shape.shape, lambda i, *_: (0, 0, 0, 0)) for shape in shapes],
            scratch_shapes=[pltpu.VMEM((rows, 2 * length), bf16)] * 2 + [pltpu.VMEM((2 * length, length), bf16)] * 2,
        ),
        out_shape=shapes,
        cost_estimate=pl.CostEstimate(
            flops=12 * rows * length * length, transcendentals=0, bytes_accessed=8 << 20
        ),
        name="spectra",
    )(ids, *received, jnp.asarray(high), jnp.asarray(low))


def gram_body(ids, bins, offsets, *refs, spans, parts, peers, devices, base, final, factor, group):
    window, refs = refs[:spans], refs[spans:]
    columns = [refs[parts * g:parts * (g + 1)] for g in range(peers)]
    refs = refs[parts * peers:]
    if final:
        before, refs = refs[0], refs[1:]
    outs, refs = (refs[:2], refs[2:]) if final else (refs[:1], refs[1:])
    extended, fresh, left_high, left_low, right_high, right_low, sums, sems, fresh_sems = refs[:9]
    k = pl.program_id(0)
    steps = pl.num_programs(0)
    size = columns[0][0].shape[0]
    sensors, length = window[0].shape[2:]
    rows = 2 * sensors
    alphas = sums.shape[0] // rows
    tiles = length // 128
    blocks = alphas // group
    each = bins.shape[0] // (2 * devices)
    here = each * devices

    def arrivals(chan, part):
        slot = lax.rem(chan, 2)
        return [
            pltpu.make_async_copy(columns[g][part].at[lax.rem(chan, size)], fresh.at[slot, g], fresh_sems.at[slot, g])
            for g in range(peers)
        ]

    def request(chan):
        for part in range(parts):

            @pl.when((chan >= part * size) & (chan < (part + 1) * size))
            def _():
                for copy in arrivals(chan, part):
                    copy.start()

    def pieces():
        copies = []
        start = 0
        for i, part in enumerate(window):
            copies.append(pltpu.make_async_copy(part, extended.at[start:start + part.shape[0]], sems.at[i]))
            start += part.shape[0]
        if final:
            copies.append(pltpu.make_async_copy(before.at[base:base + alphas], refs[9], sems.at[spans]))
        return copies

    @pl.when(k == 0)
    def _():
        request(k)
        for copy in pieces():
            copy.start()
        sums[...] = jnp.zeros(sums.shape, f32)

    for copy in arrivals(k, 0):
        copy.wait()
    request(k + 1)

    slot = lax.rem(k, 2)
    for g in range(peers):
        peer = jnp.bitwise_xor(ids[1], g)
        for c in range(2):
            high, low = split(fresh[slot, g, c])
            place = pl.ds(pl.multiple_of((c * peers + peer) * sensors, sensors), sensors)
            for t in range(tiles):
                right_high[t, place] = high[:, t * 128:(t + 1) * 128]
                right_low[t, place] = low[:, t * 128:(t + 1) * 128]

    lane = lax.broadcasted_iota(jnp.int32, (rows, 128), 1)

    def build(chan, block, slot):
        for a in range(group):
            whole = base + block * group + a
            position = lax.rem(whole, here)
            lane_group = position // each
            device = 2 * lax.rem(lane_group, devices // 2) + lane_group // (devices // 2)
            j = jnp.bitwise_xor(ids[0], device) * (2 * each) + (whole // here) * each + lax.rem(position, each)
            q = bins[j]
            source = chan + 2 * steps - offsets[j]
            tile = lax.shift_right_logical(q, 7)
            rest = jnp.bitwise_and(q, 127)
            turn = jnp.bitwise_and(128 - rest, 127)
            keep = lane < 128 - rest
            turned = []
            for t in range(tiles):
                start = pl.multiple_of(lax.rem(tile + t, tiles) * 128, 128)
                data = extended[source, :, :, pl.ds(start, 128)].reshape(rows, 128)
                turned.append(pltpu.roll(data, turn, 1))
            for t in range(tiles):
                high, low = split(jnp.where(keep, turned[t], turned[(t + 1) % tiles]))
                left_high[slot, t, a * rows:(a + 1) * rows] = high
                left_low[slot, t, a * rows:(a + 1) * rows] = low

    def joined(ref):
        return jnp.concatenate([ref[t] for t in range(tiles)], 1)

    def multiply(block, slot):
        place = pl.ds(pl.multiple_of(block * (group * rows), group * rows), group * rows)
        left = (joined(left_high.at[slot]), joined(left_low.at[slot]))
        product = dot3(left, (joined(right_high), joined(right_low)), nt_dims)
        sums[place] = sums[place] + product

    @pl.when(k == 0)
    def _():
        for copy in pieces()[:spans]:
            copy.wait()
        build(0, 0, 0)

    def pair(i, carry):
        build(k, 2 * i + 1, 1)
        multiply(2 * i, 0)
        wrap = 2 * i + 2 == blocks
        build(jnp.where(wrap, jnp.minimum(k + 1, steps - 1), k), jnp.where(wrap, 0, 2 * i + 2), 0)
        multiply(2 * i + 1, 1)
        return carry

    lax.fori_loop(0, blocks // 2, pair, 0)

    @pl.when(k == steps - 1)
    def _():
        count = outs[0].shape[3]
        extent = outs[0].shape[0]
        if final:
            pieces()[spans].wait()

        for piece, out in enumerate(outs):

            def finish(j, carry):
                position = piece * extent + j
                cross = sums[pl.ds(pl.multiple_of(position * rows, rows), rows)]
                real = cross[:sensors, :count] + cross[sensors:, count:]
                imag = cross[sensors:, :count] - cross[:sensors, count:]
                if final:
                    real = (real + refs[9][position, 0]) * factor
                    imag = (imag + refs[9][position, 1]) * factor
                out[j, 0] = real
                out[j, 1] = imag
                return carry

            lax.fori_loop(0, extent, finish, 0, unroll=4)


def gram_sums(ids, bins, offsets, window, columns, before, side, devices, factor):
    half, _, sensors, length = window[0].shape
    peers = len(columns)
    parts = len(columns[0])
    spans = len(window)
    final = before is not None
    outs = 2 if final else 1
    alphas = bins.shape[0] // outs
    count = peers * sensors
    rows = 2 * sensors
    group = min(alphas // 2, 512 // rows)
    anywhere = pl.BlockSpec(memory_space=pl.ANY)
    tiles = length // 128
    shape = (alphas // outs, 2, sensors, count)
    return pl.pallas_call(
        functools.partial(
            gram_body, spans=spans, parts=parts, peers=peers, devices=devices, base=side * alphas, final=final, factor=factor, group=group
        ),
        grid_spec=pltpu.PrefetchScalarGridSpec(
            num_scalar_prefetch=3,
            grid=(half,),
            in_specs=[anywhere] * (spans + parts * peers + outs - 1),
            out_specs=[pl.BlockSpec(shape, lambda k, *_: (0, 0, 0, 0))] * outs,
            scratch_shapes=[
                pltpu.VMEM((3 * half, 2, sensors, length), f32),
                pltpu.VMEM((2, peers, 2, sensors, length), f32),
                pltpu.VMEM((2, tiles, group * rows, 128), bf16),
                pltpu.VMEM((2, tiles, group * rows, 128), bf16),
                pltpu.VMEM((tiles, 2 * count, 128), bf16),
                pltpu.VMEM((tiles, 2 * count, 128), bf16),
                pltpu.VMEM((alphas * rows, 2 * count), f32),
                pltpu.SemaphoreType.DMA((spans + 1,)),
                pltpu.SemaphoreType.DMA((2, peers)),
            ]
            + [pltpu.VMEM((alphas, 2, sensors, count), f32)] * (outs - 1),
        ),
        out_shape=[jax.ShapeDtypeStruct(shape, f32)] * outs,
        cost_estimate=pl.CostEstimate(
            flops=6 * half * length * alphas * rows * 2 * count, transcendentals=0, bytes_accessed=8 << 20
        ),
        name="gram",
    )(ids, bins, offsets, *window, *[part for group in columns for part in group], *([before] if final else []))


def on_device(samples, bins, offsets):
    chan_count = lax.axis_size("chan")
    peers = lax.axis_size("sensor")
    channels = samples.shape[3]
    ids = jnp.stack([lax.axis_index("chan"), lax.axis_index("sensor")]).astype(jnp.int32)
    pieces = demodulate(ids, samples, chan_count)
    received = [None, None]
    for side in (1, 0):
        received[side] = [pieces[side]] + [None] * (chan_count - 1)
        for r in range(1, chan_count):
            received[side][r] = swap(pieces[2 * r + side], "chan", r)
    route = [(i, (i + 1) % chan_count) for i in range(chan_count)]
    upper_whole, *uppers = whitened(ids, received[1], 2)
    upper_rim = lax.ppermute(upper_whole, "chan", route)
    columns = [{0: part} for part in uppers]
    single = [r for r in range(1, peers) if r & (r - 1) == 0]
    for i, gathered in enumerate(columns):
        for r in single if i else single[::-1]:
            gathered[r] = swap(gathered[0], "sensor", r)
    for i, gathered in enumerate(columns):
        for r in range(1, peers):
            if r not in single:
                bits = [b for b in single if r & b]
                bit = bits[0] if i else bits[-1]
                gathered[r] = swap(gathered[r ^ bit], "sensor", bit)
    upper_columns = [[gathered[r] for gathered in columns] for r in range(peers)]
    (lower,) = whitened(ids, received[0], 0)
    lower_columns = [[lower]] + [[swap(lower, "sensor", r)] for r in range(1, peers)]
    lower_rim = lax.ppermute(lower, "chan", route)
    length = lower.shape[3]
    factor = 1.0 / math.sqrt(channels * length)
    upper_window = [upper_rim, lower] + uppers
    lower_window = [lower_rim, upper_rim, lower]
    scan = functools.partial(gram_sums, ids, bins, offsets, devices=chan_count, factor=factor)
    upper = scan(upper_window, upper_columns, None, 0)[0]
    results = []
    for side in range(2):
        same, other = scan(lower_window, lower_columns, upper, side)
        near = swap(other, "chan", 1)
        each = same.shape[0] // (chan_count // 2)
        total = None
        for q in range(chan_count // 2 - 1, -1, -1):
            place = slice(q * each, (q + 1) * each)
            both = same[place] + near[place]
            if q:
                both = swap(both, "chan", 2 * q)
            total = both if total is None else total + both
        results.append(total)
    return jnp.concatenate(results, 0)


def solution(mesh):
    return jax.shard_map(
        on_device,
        mesh=mesh,
        in_specs=(P(None, "sensor", "chan", None), P(), P()),
        out_specs=P("chan", None, "sensor", None),
        check_vma=False,
    )
```

time: 1760 us -> 240 us (0.14); the launches traced: 1730 us -> 239 us
  local copies, waits for them, and re-layouts: 1370 us -> 3.01 us
  matrix products: 173 us -> 0 us
  Pallas kernels: 0 us -> 112 us
  waiting for transfers between devices: 124 us -> 80.3 us
  other arithmetic: 39 us -> 3.5 us
  starting transfers between devices: 6.43 us -> 40.5 us
    gather x320 -> x0, local copies, waits for them, and re-layouts: 1130 us -> none
    dot_general x18 -> x0, matrix products: 173 us -> none  [the longest x16 163 us: one_block(): jnp.einsum('akp,kq->apq', left_rows, flattened, precision=lax.Precision.H...]
    reshape x20 -> x0, local copies, waits for them, and re-layouts: 157 us -> none  [the longest x16 150 us: one_alpha(): return shifted.reshape(chans * length, 2 * sensors_here)]
    pallas_call x0 -> x6, Pallas kernels: none -> 112 us  [the longest x3 94.3 us: gram_sums(): pl.pallas_call(functools.partial(gram_body, spans=spans, parts=parts, pee...]
    ppermute x1 -> x33, waiting for transfers between devices: 26 us -> 80.3 us  [the longest x31 80.3 us: swap(): return lax.ppermute(block, axis, [(i, i ^ distance) for i in range(size)])]
    ppermute x1 -> x33, starting transfers between devices: 0.01 us -> 40.5 us  [the longest x31 40.5 us: swap(): return lax.ppermute(block, axis, [(i, i ^ distance) for i in range(size)])]
    all_to_all x1 -> x0, waiting for transfers between devices: 39.9 us -> none  [on_device(): lax.all_to_all(demodulates, 'chan', split_axis=2, concat_axis=3, tiled=True)]
    reduce_scatter x1 -> x0, waiting for transfers between devices: 36.1 us -> none  [on_device(): lax.psum_scatter(partial_value, 'chan', scatter_dimension=0, tiled=True)]
  transfers between devices with their start and end apart: 4 -> 33, of which waited for: 4 -> 12; matrix products, arithmetic and copies ran while one was open for 3% -> 1% of each run, Pallas kernels for 0% -> 34%
where the time goes in v1:
time: 240 us; the launch traced here: 239 us
  Pallas kernels  112 us (47%)
  waiting for transfers between devices  80.3 us (33%)
  starting transfers between devices  40.5 us (17%)
  other arithmetic  3.5 us (1%)
  local copies, waits for them, and re-layouts  3.01 us (1%)
    pallas_call x3, Pallas kernels, gram_sums(): pl.pallas_call(functools.partial(gram_body, spans=spans, parts=parts, pee...  94.3 us
    ppermute x31, waiting for transfers between devices, swap(): return lax.ppermute(block, axis, [(i, i ^ distance) for i in range(size)])  80.3 us
    ppermute x31, starting transfers between devices, swap(): return lax.ppermute(block, axis, [(i, i ^ distance) for i in range(size)])  40.5 us
    pallas_call x2, Pallas kernels, whitened(): pl.pallas_call(functools.partial(spectra_body, sources=sources, places=pl...  11.6 us
    pallas_call x1, Pallas kernels, demodulate(): pl.pallas_call(demod_body, grid_spec=pltpu.PrefetchScalarGridSpec(num_sca...  5.76 us
  transfers between devices with their start and end apart: 33, of which 12 were waited for; matrix products, arithmetic and copies ran while one was open for 1% of the time, Pallas kernels for 34%

profile of v1, /device:TPU:0, one launch (start us, length us, event | category | flops | bytes accessed | tf_op | source)
XLA Modules:
  0.0 239.3 jit_solution(10640209448613896994)
XLA Ops:
  0.0 0.6 pad_add_fusion.ids
  0.6 5.8 %demod.1 = (f32[8,32,128]{2,1,0:T(8,128)}, f32[8,32,128]{2,1,0:T(8,128)}, f32[8,32,128]{2,1,0:T(8,128)}, f32[8,32,128]{2,1,0:T(8,128)}, f32[8,32,128]{2,1,0:T(8,...) custom-call(s32[2]{0:T(128)} %pad_add_fusion.ids, ...), custom_call_target="tpu_custom_call" | custom-call | tf_op jit(solution)/shard_map/demod/pallas_call | solution.py:85
  6.4 2.5 %collective-permute-start.10 = (f32[8,32,128]{2,1,0:T(8,128)}, f32[8,32,128]{2,1,0:T(8,128)S(1)}, u32[]{:S(2)}, u32[]{:S(2)}) collective-permute-start(f32[8,32,128]{2,1,0:T(8,128)} %get-tuple-element.39), channel_id=1, source_target_pairs={{0,3},{1,2},{2,1},{3,0},{4,7},{5,6},{6,5},{7,4},{8,11},{9,10},{10,... | collective-permute-start | bytes 393224 | tf_op jit(solution)/shard_map/ppermute | solution.py:57
  8.9 2.6 %collective-permute-start.11 = (f32[8,32,128]{2,1,0:T(8,128)}, f32[8,32,128]{2,1,0:T(8,128)S(1)}, u32[]{:S(2)}, u32[]{:S(2)}) collective-permute-start(f32[8,32,128]{2,1,0:T(8,128)} %get-tuple-element.40), channel_id=1, source_target_pairs={{0,4},{1,5},{2,6},{3,7},{4,0},{5,1},{6,2},{7,3},{8,12},{9,13},{10,... | collective-permute-start | bytes 393224 | tf_op jit(solution)/shard_map/ppermute | solution.py:57
  11.5 0.3 collective-permute-start.12
  11.9 2.5 %collective-permute-start.13 = (f32[8,32,128]{2,1,0:T(8,128)}, f32[8,32,128]{2,1,0:T(8,128)S(1)}, u32[]{:S(2)}, u32[]{:S(2)}) collective-permute-start(f32[8,32,128]{2,1,0:T(8,128)} %get-tuple-element.42), channel_id=1, source_target_pairs={{0,6},{1,7},{2,4},{3,5},{4,2},{5,3},{6,0},{7,1},{8,14},{9,15},{10,... | collective-permute-start | bytes 393224 | tf_op jit(solution)/shard_map/ppermute | solution.py:57
  14.3 0.8 collective-permute-start.14
  15.1 0.7 collective-permute-start.8
  15.8 11.8 %collective-permute-done.11.refs_4_ = f32[8,32,128]{2,1,0:T(8,128)S(1)} collective-permute-done((f32[8,32,128]{2,1,0:T(8,128)}, f32[8,32,128]{2,1,0:T(8,128)S(1)}, u32[]{:S(2)}, u32[]{:S(2)}) %collective-permute-start.11) | collective-permute-done | bytes 131104 | tf_op jit(solution)/shard_map/ppermute | solution.py:57
  27.6 0.0 collective-permute-start.9
  27.7 2.3 collective-permute-done.12.refs_5_
  30.0 0.3 collective-permute-start
  30.3 0.0 collective-permute-done.8.refs_1_
  30.4 2.6 %collective-permute-done.9.refs_2_ = f32[8,32,128]{2,1,0:T(8,128)S(1)} collective-permute-done((f32[8,32,128]{2,1,0:T(8,128)}, f32[8,32,128]{2,1,0:T(8,128)S(1)}, u32[]{:S(2)}, u32[]{:S(2)}) %collective-permute-start.9) | collective-permute-done | bytes 131104 | tf_op jit(solution)/shard_map/ppermute | solution.py:57
  33.0 0.6 copy-done.24
  33.7 6.1 %spectra.3 = (f32[8,2,32,512]{3,2,1,0:T(8,128)}, f32[4,2,32,512]{3,2,1,0:T(8,128)}, f32[4,2,32,512]{3,2,1,0:T(8,128)}) custom-call(s32[2]{0:T(128)} %pad_add_fusion.ids, f32[8,32,128]{2,1,0:T(8,128)} %get-tuple-element.36.refs_0_, f32[8,32,128]{2,1,0:T(8,128)} %copy-done.22, f32[8,32,128]{2,1,0:T(8,128)} %copy-done.24, f32[8,32,128]{2,1,0:T(8,128)} %copy-done.15, ...), custom_call_target="tpu_custom_call" | custom-call | flops 1610612736 | bytes 8388608 | tf_op jit(solution)/shard_map/spectra/pallas_call | solution.py:135
  39.7 1.5 collective-permute-start.19
  41.3 1.5 collective-permute-start.22
  42.8 0.0 collective-permute-start.15
  42.8 3.2 %collective-permute-start.1 = (f32[8,32,128]{2,1,0:T(8,128)S(1)}, f32[8,32,128]{2,1,0:T(8,128)S(1)}, u32[]{:S(2)}, u32[]{:S(2)}) collective-permute-start(f32[8,32,128]{2,1,0:T(8,128)S(1)} %copy-done.11), channel_id=1, source_target_pairs={{0,2},{1,3},{2,0},{3,1},{4,6},{5,7},{6,4},{7,5},{8,10},{9,11},{10,... | collective-permute-start | bytes 393224 | tf_op jit(solution)/shard_map/ppermute | solution.py:57
  46.0 1.5 collective-permute-start.2
  47.5 6.7 %collective-permute-done.1.refs_2_ = f32[8,32,128]{2,1,0:T(8,128)S(1)} collective-permute-done((f32[8,32,128]{2,1,0:T(8,128)S(1)}, f32[8,32,128]{2,1,0:T(8,128)S(1)}, u32[]{:S(2)}, u32[]{:S(2)}) %collective-permute-start.1) | collective-permute-done | bytes 131104 | tf_op jit(solution)/shard_map/ppermute | solution.py:57
  54.2 0.0 collective-permute-start.3
  54.2 11.5 %collective-permute-done.2.refs_3_ = f32[8,32,128]{2,1,0:T(8,128)S(1)} collective-permute-done((f32[8,32,128]{2,1,0:T(8,128)S(1)}, f32[8,32,128]{2,1,0:T(8,128)S(1)}, u32[]{:S(2)}, u32[]{:S(2)}) %collective-permute-start.2) | collective-permute-done | bytes 131104 | tf_op jit(solution)/shard_map/ppermute | solution.py:57
  65.8 0.2 collective-permute-start.4
  66.0 2.1 collective-permute-start.5
  68.1 9.1 %collective-permute-done.4.refs_5_ = f32[8,32,128]{2,1,0:T(8,128)S(1)} collective-permute-done((f32[8,32,128]{2,1,0:T(8,128)S(1)}, f32[8,32,128]{2,1,0:T(8,128)S(1)}, u32[]{:S(2)}, u32[]{:S(2)}) %collective-permute-start.4) | collective-permute-done | bytes 131104 | tf_op jit(solution)/shard_map/ppermute | solution.py:57
  77.2 0.9 collective-permute-start.6
  78.1 0.6 collective-permute-start.20
  78.7 6.0 %collective-permute-done.6.refs_7_ = f32[8,32,128]{2,1,0:T(8,128)S(1)} collective-permute-done((f32[8,32,128]{2,1,0:T(8,128)S(1)}, f32[8,32,128]{2,1,0:T(8,128)S(1)}, u32[]{:S(2)}, u32[]{:S(2)}) %collective-permute-start.6) | collective-permute-done | bytes 131104 | tf_op jit(solution)/shard_map/ppermute | solution.py:57
  84.6 0.5 collective-permute-start.21
  85.1 1.5 collective-permute-start.23
  86.7 0.6 collective-permute-start.24
  87.3 5.6 %spectra.2.refs_1_.refs_2_.refs_3_ = f32[8,2,32,512]{3,2,1,0:T(8,128)} custom-call(s32[2]{0:T(128)} %pad_add_fusion.ids, f32[8,32,128]{2,1,0:T(8,128)} %get-tuple-element.28.refs_0_, f32[8,32,128]{2,1,0:T(8,128)} %copy-done.9, f32[8,32,128]{2,1,0:T(8,128)} %copy-done.12, f32[8,32,128]{2,1,0:T(8,128)} %copy-done.13, f32[8,32,128]{2,1,0:T(8,128)} %copy-done.14, ...), custom_call_target="tpu_custom_call" | custom-call | flops 1610612736 | bytes 8388608 | tf_op jit(solution)/shard_map/spectra/pallas_call | solution.py:135
  92.8 1.5 collective-permute-start.16
  94.4 5.4 %collective-permute-done.21.refs_8_ = f32[4,2,32,512]{3,2,1,0:T(8,128)} collective-permute-done((f32[4,2,32,512]{3,2,1,0:T(8,128)}, f32[4,2,32,512]{3,2,1,0:T(8,128)}, u32[]{:S(2)}, u32[]{:S(2)}) %collective-permute-start.21) | collective-permute-done | bytes 524320 | tf_op jit(solution)/shard_map/ppermute | solution.py:57
  99.7 0.5 collective-permute-start.17
  100.2 10.7 %collective-permute-done.23.refs_10_ = f32[4,2,32,512]{3,2,1,0:T(8,128)} collective-permute-done((f32[4,2,32,512]{3,2,1,0:T(8,128)}, f32[4,2,32,512]{3,2,1,0:T(8,128)}, u32[]{:S(2)}, u32[]{:S(2)}) %collective-permute-start.23) | collective-permute-done | bytes 524320 | tf_op jit(solution)/shard_map/ppermute | solution.py:57
  111.0 0.5 collective-permute-start.18
  111.4 0.0 collective-permute-done.24.refs_11_
  111.4 0.0 collective-permute-start.7
  111.5 0.0 collective-permute-done.15.refs_0_.refs_1_
  111.5 1.0 copy-done.1
  112.5 44.7 %gram.3.refs_7_ = f32[64,2,32,128]{3,2,1,0:T(8,128)} custom-call(s32[2]{0:T(128)} %pad_add_fusion.ids, s32[64]{0:T(128)} %bins.5, s32[64]{0:T(128)} %offsets.5, f32[8,2,32,512]{3,2,1,0:T(8,128)} %copy-done.1, f32[8,2,32,512]{3,2,1,0:T(8,128)} %spectra.2.refs_1_.refs_2_.refs_3_, f32[4,2,32,512]{3,2,1,0:T(8,128)} %get-tuple-element.45.refs_2_.refs_4_, ...), custom_call_target="tpu_custom_call" | custom-call | flops 25769803776 | bytes 8388608 | tf_op jit(solution)/shard_map/gram/pallas_call | solution.py:306
  157.3 0.9 copy-done.2
  158.2 0.4 copy-done.3
  158.6 24.9 %gram.4 = (f32[16,2,32,128]{3,2,1,0:T(8,128)}, f32[16,2,32,128]{3,2,1,0:T(8,128)}) custom-call(s32[2]{0:T(128)} %pad_add_fusion.ids, s32[64]{0:T(128)} %bins.5, s32[64]{0:T(128)} %offsets.5, f32[8,2,32,512]{3,2,1,0:T(8,128)} %collective-permute-done.7.refs_0_, f32[8,2,32,512]{3,2,1,0:T(8,128)} %copy-done.1, ...), custom_call_target="tpu_custom_call" | custom-call | flops 12884901888 | bytes 8388608 | tf_op jit(solution)/shard_map/gram/pallas_call | solution.py:306
  183.5 3.1 %collective-permute-start.25 = (f32[16,2,32,128]{3,2,1,0:T(8,128)}, f32[16,2,32,128]{3,2,1,0:T(8,128)S(1)}, u32[]{:S(2)}, u32[]{:S(2)}) collective-permute-start(f32[16,2,32,128]{3,2,1,0:T(8,128)} %get-tuple-element.48), channel_id=1, source_target_pairs={{0,1},{1,0},{2,3},{3,2},{4,5},{5,4},{6,7},{7,6},{8,9},{9,8},{10,11... | collective-permute-start | bytes 1572872 | tf_op jit(solution)/shard_map/ppermute | solution.py:57
  186.6 24.7 %gram.5 = (f32[16,2,32,128]{3,2,1,0:T(8,128)}, f32[16,2,32,128]{3,2,1,0:T(8,128)}) custom-call(s32[2]{0:T(128)} %pad_add_fusion.ids, s32[64]{0:T(128)} %bins.5, s32[64]{0:T(128)} %offsets.5, f32[8,2,32,512]{3,2,1,0:T(8,128)} %collective-permute-done.7.refs_0_, f32[8,2,32,512]{3,2,1,0:T(8,128)} %copy-done.1, ...), custom_call_target="tpu_custom_call" | custom-call | flops 12884901888 | bytes 8388608 | tf_op jit(solution)/shard_map/gram/pallas_call | solution.py:306
  211.3 0.2 collective-permute-start.29
  211.6 0.1 slice_add_fusion.6
  211.6 0.9 collective-permute-start.26
  212.5 1.7 collective-permute-start.27
  214.2 1.9 collective-permute-start.28
  216.1 1.1 slice_add_fusion.2
  217.2 0.9 collective-permute-start.30
  218.1 0.8 collective-permute-start.31
  218.8 1.2 collective-permute-done.26
  220.0 4.7 %collective-permute-start.32 = (f32[4,2,32,128]{3,2,1,0:T(8,128)S(1)}, f32[4,2,32,128]{3,2,1,0:T(8,128)S(1)}, u32[]{:S(2)}, u32[]{:S(2)}) collective-permute-start(f32[4,2,32,128]{3,2,1,0:T(8,128)S(1)} %get-tuple-element.55), channel_id=1, source_target_pairs={{0,2},{1,3},{2,0},{3,1},{4,6},{5,7},{6,4},{7,5},{8,10},{9,11},{10,... | collective-permute-start | bytes 393224 | tf_op jit(solution)/shard_map/ppermute | solution.py:57
  224.7 7.9 %collective-permute-done.27 = f32[4,2,32,128]{3,2,1,0:T(8,128)S(1)} collective-permute-done((f32[4,2,32,128]{3,2,1,0:T(8,128)S(1)}, f32[4,2,32,128]{3,2,1,0:T(8,128)S(1)}, u32[]{:S(2)}, u32[]{:S(2)}) %collective-permute-start.27) | collective-permute-done | bytes 131104 | tf_op jit(solution)/shard_map/ppermute | solution.py:57
  232.6 0.1 fusion.1
  232.7 4.9 %collective-permute-done.31 = f32[4,2,32,128]{3,2,1,0:T(8,128)S(1)} collective-permute-done((f32[4,2,32,128]{3,2,1,0:T(8,128)S(1)}, f32[4,2,32,128]{3,2,1,0:T(8,128)S(1)}, u32[]{:S(2)}, u32[]{:S(2)}) %collective-permute-start.31) | collective-permute-done | bytes 131104 | tf_op jit(solution)/shard_map/ppermute | solution.py:57
  237.6 1.0 fusion
  238.6 0.7 pad_maximum_fusion
  (64 shorter events, 0.1 us)
Async XLA Ops:
  6.4 8.7 %collective-permute-start.10 = (f32[8,32,128]{2,1,0:T(8,128)}, f32[8,32,128]{2,1,0:T(8,128)S(1)}, u32[]{:S(2)}, u32[]{:S(2)}) collective-permute-start(f32[8,32,128]{2,1,0:T(8,128)} %get-tuple-element.39), channel_id=1, source_target_pairs={{0,3},{1,2},{2,1},{3,0},{4,7},{5,6},{6,5},{7,4},{8,11},{9,10},{10,... | collective-permute-start | bytes 393224 | tf_op jit(solution)/shard_map/ppermute | solution.py:57
  8.9 18.7 %collective-permute-start.11 = (f32[8,32,128]{2,1,0:T(8,128)}, f32[8,32,128]{2,1,0:T(8,128)S(1)}, u32[]{:S(2)}, u32[]{:S(2)}) collective-permute-start(f32[8,32,128]{2,1,0:T(8,128)} %get-tuple-element.40), channel_id=1, source_target_pairs={{0,4},{1,5},{2,6},{3,7},{4,0},{5,1},{6,2},{7,3},{8,12},{9,13},{10,... | collective-permute-start | bytes 393224 | tf_op jit(solution)/shard_map/ppermute | solution.py:57
  11.5 18.5 %collective-permute-start.12 = (f32[8,32,128]{2,1,0:T(8,128)}, f32[8,32,128]{2,1,0:T(8,128)S(1)}, u32[]{:S(2)}, u32[]{:S(2)}) collective-permute-start(f32[8,32,128]{2,1,0:T(8,128)} %get-tuple-element.41), channel_id=1, source_target_pairs={{0,5},{1,4},{2,7},{3,6},{4,1},{5,0},{6,3},{7,2},{8,13},{9,12},{10,... | collective-permute-start | bytes 393224 | tf_op jit(solution)/shard_map/ppermute | solution.py:57
  11.9 18.4 %collective-permute-start.13 = (f32[8,32,128]{2,1,0:T(8,128)}, f32[8,32,128]{2,1,0:T(8,128)S(1)}, u32[]{:S(2)}, u32[]{:S(2)}) collective-permute-start(f32[8,32,128]{2,1,0:T(8,128)} %get-tuple-element.42), channel_id=1, source_target_pairs={{0,6},{1,7},{2,4},{3,5},{4,2},{5,3},{6,0},{7,1},{8,14},{9,15},{10,... | collective-permute-start | bytes 393224 | tf_op jit(solution)/shard_map/ppermute | solution.py:57
  14.3 16.0 %collective-permute-start.14 = (f32[8,32,128]{2,1,0:T(8,128)}, f32[8,32,128]{2,1,0:T(8,128)S(1)}, u32[]{:S(2)}, u32[]{:S(2)}) collective-permute-start(f32[8,32,128]{2,1,0:T(8,128)} %get-tuple-element.43), channel_id=1, source_target_pairs={{0,7},{1,6},{2,5},{3,4},{4,3},{5,2},{6,1},{7,0},{8,15},{9,14},{10,... | collective-permute-start | bytes 393224 | tf_op jit(solution)/shard_map/ppermute | solution.py:57
  15.1 17.9 %copy-start.15 = (f32[8,32,128]{2,1,0:T(8,128)}, f32[8,32,128]{2,1,0:T(8,128)S(1)}, u32[]{:S(2)}) copy-start(f32[8,32,128]{2,1,0:T(8,128)S(1)} %collective-permute-done.10.refs_3_) | copy-start | bytes 393220
  15.1 15.2 %collective-permute-start.8 = (f32[8,32,128]{2,1,0:T(8,128)}, f32[8,32,128]{2,1,0:T(8,128)S(1)}, u32[]{:S(2)}, u32[]{:S(2)}) collective-permute-start(f32[8,32,128]{2,1,0:T(8,128)} %get-tuple-element.37), channel_id=1, source_target_pairs={{0,1},{1,0},{2,3},{3,2},{4,5},{5,4},{6,7},{7,6},{8,9},{9,8},{10,11... | collective-permute-start | bytes 393224 | tf_op jit(solution)/shard_map/ppermute | solution.py:57
  27.6 5.3 %copy-start.16 = (f32[8,32,128]{2,1,0:T(8,128)}, f32[8,32,128]{2,1,0:T(8,128)S(1)}, u32[]{:S(2)}) copy-start(f32[8,32,128]{2,1,0:T(8,128)S(1)} %collective-permute-done.11.refs_4_) | copy-start | bytes 393220
  27.6 5.3 %collective-permute-start.9 = (f32[8,32,128]{2,1,0:T(8,128)}, f32[8,32,128]{2,1,0:T(8,128)S(1)}, u32[]{:S(2)}, u32[]{:S(2)}) collective-permute-start(f32[8,32,128]{2,1,0:T(8,128)} %get-tuple-element.38), channel_id=1, source_target_pairs={{0,2},{1,3},{2,0},{3,1},{4,6},{5,7},{6,4},{7,5},{8,10},{9,11},{10,... | collective-permute-start | bytes 393224 | tf_op jit(solution)/shard_map/ppermute | solution.py:57
  30.0 3.0 %copy-start.17 = (f32[8,32,128]{2,1,0:T(8,128)}, f32[8,32,128]{2,1,0:T(8,128)S(1)}, u32[]{:S(2)}) copy-start(f32[8,32,128]{2,1,0:T(8,128)S(1)} %collective-permute-done.12.refs_5_) | copy-start | bytes 393220
  30.0 16.0 %collective-permute-start = (f32[8,32,128]{2,1,0:T(8,128)}, f32[8,32,128]{2,1,0:T(8,128)S(1)}, u32[]{:S(2)}, u32[]{:S(2)}) collective-permute-start(f32[8,32,128]{2,1,0:T(8,128)} %get-tuple-element.29), channel_id=1, source_target_pairs={{0,1},{1,0},{2,3},{3,2},{4,5},{5,4},{6,7},{7,6},{8,9},{9,8},{10,11... | collective-permute-start | bytes 393224 | tf_op jit(solution)/shard_map/ppermute | solution.py:57
  30.3 2.7 %copy-start.19 = (f32[8,32,128]{2,1,0:T(8,128)}, f32[8,32,128]{2,1,0:T(8,128)S(1)}, u32[]{:S(2)}) copy-start(f32[8,32,128]{2,1,0:T(8,128)S(1)} %collective-permute-done.13.refs_6_) | copy-start | bytes 393220
  30.3 2.7 %copy-start.20 = (f32[8,32,128]{2,1,0:T(8,128)}, f32[8,32,128]{2,1,0:T(8,128)S(1)}, u32[]{:S(2)}) copy-start(f32[8,32,128]{2,1,0:T(8,128)S(1)} %collective-permute-done.14.refs_7_) | copy-start | bytes 393220
  30.3 2.7 %copy-start.22 = (f32[8,32,128]{2,1,0:T(8,128)}, f32[8,32,128]{2,1,0:T(8,128)S(1)}, u32[]{:S(2)}) copy-start(f32[8,32,128]{2,1,0:T(8,128)S(1)} %collective-permute-done.8.refs_1_) | copy-start | bytes 393220
  33.0 0.6 copy-start.24
  33.6 9.2 %copy-start.11 = (f32[8,32,128]{2,1,0:T(8,128)S(1)}, f32[8,32,128]{2,1,0:T(8,128)}, u32[]{:S(2)}) copy-start(f32[8,32,128]{2,1,0:T(8,128)} %get-tuple-element.30) | copy-start | bytes 393220
  33.6 12.4 %copy-start.10 = (f32[8,32,128]{2,1,0:T(8,128)S(1)}, f32[8,32,128]{2,1,0:T(8,128)}, u32[]{:S(2)}) copy-start(f32[8,32,128]{2,1,0:T(8,128)} %get-tuple-element.31) | copy-start | bytes 393220
  33.6 20.6 %copy-start.8 = (f32[8,32,128]{2,1,0:T(8,128)S(1)}, f32[8,32,128]{2,1,0:T(8,128)}, u32[]{:S(2)}) copy-start(f32[8,32,128]{2,1,0:T(8,128)} %get-tuple-element.32) | copy-start | bytes 393220
  33.6 32.2 %copy-start.7 = (f32[8,32,128]{2,1,0:T(8,128)S(1)}, f32[8,32,128]{2,1,0:T(8,128)}, u32[]{:S(2)}) copy-start(f32[8,32,128]{2,1,0:T(8,128)} %get-tuple-element.33) | copy-start | bytes 393220
  33.6 32.4 %copy-start.6 = (f32[8,32,128]{2,1,0:T(8,128)S(1)}, f32[8,32,128]{2,1,0:T(8,128)}, u32[]{:S(2)}) copy-start(f32[8,32,128]{2,1,0:T(8,128)} %get-tuple-element.34) | copy-start | bytes 393220
  33.6 43.6 %copy-start.5 = (f32[8,32,128]{2,1,0:T(8,128)S(1)}, f32[8,32,128]{2,1,0:T(8,128)}, u32[]{:S(2)}) copy-start(f32[8,32,128]{2,1,0:T(8,128)} %get-tuple-element.35) | copy-start | bytes 393220
  39.7 45.4 %collective-permute-start.19 = (f32[4,2,32,512]{3,2,1,0:T(8,128)}, f32[4,2,32,512]{3,2,1,0:T(8,128)}, u32[]{:S(2)}, u32[]{:S(2)}) collective-permute-start(f32[4,2,32,512]{3,2,1,0:T(8,128)} %get-tuple-element.45.refs_2_.refs_4_), channel_id=1, source_target_pairs={{0,8},{8,0},{16,24},{24,16},{1,9},{9,1},{17,25},{25,17},{2,10},{10... | collective-permute-start | bytes 1572872 | tf_op jit(solution)/shard_map/ppermute | solution.py:57
  41.3 45.4 %collective-permute-start.22 = (f32[4,2,32,512]{3,2,1,0:T(8,128)}, f32[4,2,32,512]{3,2,1,0:T(8,128)}, u32[]{:S(2)}, u32[]{:S(2)}) collective-permute-start(f32[4,2,32,512]{3,2,1,0:T(8,128)} %get-tuple-element.46.refs_3_.refs_5_), channel_id=1, source_target_pairs={{0,16},{8,24},{16,0},{24,8},{1,17},{9,25},{17,1},{25,9},{2,18},{10... | collective-permute-start | bytes 1572872 | tf_op jit(solution)/shard_map/ppermute | solution.py:57
  42.8 68.7 %collective-permute-start.15 = (f32[8,2,32,512]{3,2,1,0:T(8,128)}, f32[8,2,32,512]{3,2,1,0:T(8,128)S(1)}, u32[]{:S(2)}, u32[]{:S(2)}) collective-permute-start(f32[8,2,32,512]{3,2,1,0:T(8,128)} %get-tuple-element.44), channel_id=1, source_target_pairs={{0,1},{1,2},{2,3},{3,4},{4,5},{5,6},{6,7},{7,0},{8,9},{9,10},{10,1... | collective-permute-start | bytes 3145736 | tf_op jit(solution)/shard_map/ppermute | solution.py:349
  42.8 11.5 %collective-permute-start.1 = (f32[8,32,128]{2,1,0:T(8,128)S(1)}, f32[8,32,128]{2,1,0:T(8,128)S(1)}, u32[]{:S(2)}, u32[]{:S(2)}) collective-permute-start(f32[8,32,128]{2,1,0:T(8,128)S(1)} %copy-done.11), channel_id=1, source_target_pairs={{0,2},{1,3},{2,0},{3,1},{4,6},{5,7},{6,4},{7,5},{8,10},{9,11},{10,... | collective-permute-start | bytes 393224 | tf_op jit(solution)/shard_map/ppermute | solution.py:57
  46.0 41.2 %copy-start.9 = (f32[8,32,128]{2,1,0:T(8,128)}, f32[8,32,128]{2,1,0:T(8,128)S(1)}, u32[]{:S(2)}) copy-start(f32[8,32,128]{2,1,0:T(8,128)S(1)} %collective-permute-done.refs_1_) | copy-start | bytes 393220
  46.0 19.8 %collective-permute-start.2 = (f32[8,32,128]{2,1,0:T(8,128)S(1)}, f32[8,32,128]{2,1,0:T(8,128)S(1)}, u32[]{:S(2)}, u32[]{:S(2)}) collective-permute-start(f32[8,32,128]{2,1,0:T(8,128)S(1)} %copy-done.10), channel_id=1, source_target_pairs={{0,3},{1,2},{2,1},{3,0},{4,7},{5,6},{6,5},{7,4},{8,11},{9,10},{10,... | collective-permute-start | bytes 393224 | tf_op jit(solution)/shard_map/ppermute | solution.py:57
  54.2 33.0 %copy-start.12 = (f32[8,32,128]{2,1,0:T(8,128)}, f32[8,32,128]{2,1,0:T(8,128)S(1)}, u32[]{:S(2)}) copy-start(f32[8,32,128]{2,1,0:T(8,128)S(1)} %collective-permute-done.1.refs_2_) | copy-start | bytes 393220
  54.2 11.8 %collective-permute-start.3 = (f32[8,32,128]{2,1,0:T(8,128)S(1)}, f32[8,32,128]{2,1,0:T(8,128)S(1)}, u32[]{:S(2)}, u32[]{:S(2)}) collective-permute-start(f32[8,32,128]{2,1,0:T(8,128)S(1)} %copy-done.8), channel_id=1, source_target_pairs={{0,4},{1,5},{2,6},{3,7},{4,0},{5,1},{6,2},{7,3},{8,12},{9,13},{10,... | collective-permute-start | bytes 393224 | tf_op jit(solution)/shard_map/ppermute | solution.py:57
  65.8 21.4 %copy-start.13 = (f32[8,32,128]{2,1,0:T(8,128)}, f32[8,32,128]{2,1,0:T(8,128)S(1)}, u32[]{:S(2)}) copy-start(f32[8,32,128]{2,1,0:T(8,128)S(1)} %collective-permute-done.2.refs_3_) | copy-start | bytes 393220
  65.8 11.4 %collective-permute-start.4 = (f32[8,32,128]{2,1,0:T(8,128)S(1)}, f32[8,32,128]{2,1,0:T(8,128)S(1)}, u32[]{:S(2)}, u32[]{:S(2)}) collective-permute-start(f32[8,32,128]{2,1,0:T(8,128)S(1)} %copy-done.7), channel_id=1, source_target_pairs={{0,5},{1,4},{2,7},{3,6},{4,1},{5,0},{6,3},{7,2},{8,13},{9,12},{10,... | collective-permute-start | bytes 393224 | tf_op jit(solution)/shard_map/ppermute | solution.py:57
  66.0 21.2 %copy-start.14 = (f32[8,32,128]{2,1,0:T(8,128)}, f32[8,32,128]{2,1,0:T(8,128)S(1)}, u32[]{:S(2)}) copy-start(f32[8,32,128]{2,1,0:T(8,128)S(1)} %collective-permute-done.3.refs_4_) | copy-start | bytes 393220
  66.0 12.1 %collective-permute-start.5 = (f32[8,32,128]{2,1,0:T(8,128)S(1)}, f32[8,32,128]{2,1,0:T(8,128)S(1)}, u32[]{:S(2)}, u32[]{:S(2)}) collective-permute-start(f32[8,32,128]{2,1,0:T(8,128)S(1)} %copy-done.6), channel_id=1, source_target_pairs={{0,6},{1,7},{2,4},{3,5},{4,2},{5,3},{6,0},{7,1},{8,14},{9,15},{10,... | collective-permute-start | bytes 393224 | tf_op jit(solution)/shard_map/ppermute | solution.py:57
  77.2 10.0 %copy-start.18 = (f32[8,32,128]{2,1,0:T(8,128)}, f32[8,32,128]{2,1,0:T(8,128)S(1)}, u32[]{:S(2)}) copy-start(f32[8,32,128]{2,1,0:T(8,128)S(1)} %collective-permute-done.4.refs_5_) | copy-start | bytes 393220
  77.2 7.4 %collective-permute-start.6 = (f32[8,32,128]{2,1,0:T(8,128)S(1)}, f32[8,32,128]{2,1,0:T(8,128)S(1)}, u32[]{:S(2)}, u32[]{:S(2)}) collective-permute-start(f32[8,32,128]{2,1,0:T(8,128)S(1)} %copy-done.5), channel_id=1, source_target_pairs={{0,7},{1,6},{2,5},{3,4},{4,3},{5,2},{6,1},{7,0},{8,15},{9,14},{10,... | collective-permute-start | bytes 393224 | tf_op jit(solution)/shard_map/ppermute | solution.py:57
  78.1 9.1 %copy-start.21 = (f32[8,32,128]{2,1,0:T(8,128)}, f32[8,32,128]{2,1,0:T(8,128)S(1)}, u32[]{:S(2)}) copy-start(f32[8,32,128]{2,1,0:T(8,128)S(1)} %collective-permute-done.5.refs_6_) | copy-start | bytes 393220
  78.1 14.7 %collective-permute-start.20 = (f32[4,2,32,512]{3,2,1,0:T(8,128)}, f32[4,2,32,512]{3,2,1,0:T(8,128)S(1)}, u32[]{:S(2)}, u32[]{:S(2)}) collective-permute-start(f32[4,2,32,512]{3,2,1,0:T(8,128)} %get-tuple-element.46.refs_3_.refs_5_), channel_id=1, source_target_pairs={{0,8},{8,0},{16,24},{24,16},{1,9},{9,1},{17,25},{25,17},{2,10},{10... | collective-permute-start | bytes 1572872 | tf_op jit(solution)/shard_map/ppermute | solution.py:57
  84.6 2.6 %copy-start.23 = (f32[8,32,128]{2,1,0:T(8,128)}, f32[8,32,128]{2,1,0:T(8,128)S(1)}, u32[]{:S(2)}) copy-start(f32[8,32,128]{2,1,0:T(8,128)S(1)} %collective-permute-done.6.refs_7_) | copy-start | bytes 393220
  84.6 15.1 %collective-permute-start.21 = (f32[4,2,32,512]{3,2,1,0:T(8,128)}, f32[4,2,32,512]{3,2,1,0:T(8,128)}, u32[]{:S(2)}, u32[]{:S(2)}) collective-permute-start(f32[4,2,32,512]{3,2,1,0:T(8,128)} %get-tuple-element.45.refs_2_.refs_4_), channel_id=1, source_target_pairs={{0,16},{8,24},{16,0},{24,8},{1,17},{9,25},{17,1},{25,9},{2,18},{10... | collective-permute-start | bytes 1572872 | tf_op jit(solution)/shard_map/ppermute | solution.py:57
  85.1 25.8 %collective-permute-start.23 = (f32[4,2,32,512]{3,2,1,0:T(8,128)}, f32[4,2,32,512]{3,2,1,0:T(8,128)}, u32[]{:S(2)}, u32[]{:S(2)}) collective-permute-start(f32[4,2,32,512]{3,2,1,0:T(8,128)} %collective-permute-done.19.refs_6_), channel_id=1, source_target_pairs={{0,16},{8,24},{16,0},{24,8},{1,17},{9,25},{17,1},{25,9},{2,18},{10... | collective-permute-start | bytes 1572872 | tf_op jit(solution)/shard_map/ppermute | solution.py:57
  86.7 24.8 %collective-permute-start.24 = (f32[4,2,32,512]{3,2,1,0:T(8,128)}, f32[4,2,32,512]{3,2,1,0:T(8,128)}, u32[]{:S(2)}, u32[]{:S(2)}) collective-permute-start(f32[4,2,32,512]{3,2,1,0:T(8,128)} %collective-permute-done.22.refs_9_), channel_id=1, source_target_pairs={{0,8},{8,0},{16,24},{24,16},{1,9},{9,1},{17,25},{25,17},{2,10},{10... | collective-permute-start | bytes 1572872 | tf_op jit(solution)/shard_map/ppermute | solution.py:57
  92.8 1.5 copy-start.4
  92.8 64.4 %collective-permute-start.16 = (f32[8,2,32,512]{3,2,1,0:T(8,128)}, f32[8,2,32,512]{3,2,1,0:T(8,128)S(1)}, u32[]{:S(2)}, u32[]{:S(2)}) collective-permute-start(f32[8,2,32,512]{3,2,1,0:T(8,128)} %spectra.2.refs_1_.refs_2_.refs_3_), channel_id=1, source_target_pairs={{0,8},{8,0},{16,24},{24,16},{1,9},{9,1},{17,25},{25,17},{2,10},{10... | collective-permute-start | bytes 3145736 | tf_op jit(solution)/shard_map/ppermute | solution.py:57
  99.7 57.5 %collective-permute-start.17 = (f32[8,2,32,512]{3,2,1,0:T(8,128)}, f32[8,2,32,512]{3,2,1,0:T(8,128)S(1)}, u32[]{:S(2)}, u32[]{:S(2)}) collective-permute-start(f32[8,2,32,512]{3,2,1,0:T(8,128)} %spectra.2.refs_1_.refs_2_.refs_3_), channel_id=1, source_target_pairs={{0,16},{8,24},{16,0},{24,8},{1,17},{9,25},{17,1},{25,9},{2,18},{10... | collective-permute-start | bytes 3145736 | tf_op jit(solution)/shard_map/ppermute | solution.py:57
  111.0 46.3 %collective-permute-start.18 = (f32[8,2,32,512]{3,2,1,0:T(8,128)}, f32[8,2,32,512]{3,2,1,0:T(8,128)}, u32[]{:S(2)}, u32[]{:S(2)}) collective-permute-start(f32[8,2,32,512]{3,2,1,0:T(8,128)} %spectra.2.refs_1_.refs_2_.refs_3_), channel_id=1, source_target_pairs={{0,24},{8,16},{16,8},{24,0},{1,25},{9,17},{17,9},{25,1},{2,26},{10... | collective-permute-start | bytes 3145736 | tf_op jit(solution)/shard_map/ppermute | solution.py:57
  111.4 45.8 %collective-permute-start.7 = (f32[8,2,32,512]{3,2,1,0:T(8,128)}, f32[8,2,32,512]{3,2,1,0:T(8,128)}, u32[]{:S(2)}, u32[]{:S(2)}) collective-permute-start(f32[8,2,32,512]{3,2,1,0:T(8,128)} %spectra.2.refs_1_.refs_2_.refs_3_), channel_id=1, source_target_pairs={{0,1},{1,2},{2,3},{3,4},{4,5},{5,6},{6,7},{7,0},{8,9},{9,10},{10,1... | collective-permute-start | bytes 3145736 | tf_op jit(solution)/shard_map/ppermute | solution.py:364
  111.5 1.0 copy-start.1
  157.2 1.0 copy-start.2
  157.2 1.4 copy-start.3
  183.5 28.1 %copy-start = (f32[16,2,32,128]{3,2,1,0:T(8,128)S(1)}, f32[16,2,32,128]{3,2,1,0:T(8,128)}, u32[]{:S(2)}) copy-start(f32[16,2,32,128]{3,2,1,0:T(8,128)} %get-tuple-element.47) | copy-start | bytes 1572868
  183.5 28.1 %collective-permute-start.25 = (f32[16,2,32,128]{3,2,1,0:T(8,128)}, f32[16,2,32,128]{3,2,1,0:T(8,128)S(1)}, u32[]{:S(2)}, u32[]{:S(2)}) collective-permute-start(f32[16,2,32,128]{3,2,1,0:T(8,128)} %get-tuple-element.48), channel_id=1, source_target_pairs={{0,1},{1,0},{2,3},{3,2},{4,5},{5,4},{6,7},{7,6},{8,9},{9,8},{10,11... | collective-permute-start | bytes 1572872 | tf_op jit(solution)/shard_map/ppermute | solution.py:57
  211.3 4.8 %collective-permute-start.29 = (f32[16,2,32,128]{3,2,1,0:T(8,128)}, f32[16,2,32,128]{3,2,1,0:T(8,128)S(1)}, u32[]{:S(2)}, u32[]{:S(2)}) collective-permute-start(f32[16,2,32,128]{3,2,1,0:T(8,128)} %get-tuple-element.50), channel_id=1, source_target_pairs={{0,1},{1,0},{2,3},{3,2},{4,5},{5,4},{6,7},{7,6},{8,9},{9,8},{10,11... | collective-permute-start | bytes 1572872 | tf_op jit(solution)/shard_map/ppermute | solution.py:57
  211.6 8.4 %collective-permute-start.26 = (f32[4,2,32,128]{3,2,1,0:T(8,128)S(1)}, f32[4,2,32,128]{3,2,1,0:T(8,128)S(1)}, u32[]{:S(2)}, u32[]{:S(2)}) collective-permute-start(f32[4,2,32,128]{3,2,1,0:T(8,128)S(1)} %get-tuple-element.53), channel_id=1, source_target_pairs={{0,6},{1,7},{2,4},{3,5},{4,2},{5,3},{6,0},{7,1},{8,14},{9,15},{10,... | collective-permute-start | bytes 393224 | tf_op jit(solution)/shard_map/ppermute | solution.py:57
  212.5 20.1 %collective-permute-start.27 = (f32[4,2,32,128]{3,2,1,0:T(8,128)S(1)}, f32[4,2,32,128]{3,2,1,0:T(8,128)S(1)}, u32[]{:S(2)}, u32[]{:S(2)}) collective-permute-start(f32[4,2,32,128]{3,2,1,0:T(8,128)S(1)} %get-tuple-element.51), channel_id=1, source_target_pairs={{0,4},{1,5},{2,6},{3,7},{4,0},{5,1},{6,2},{7,3},{8,12},{9,13},{10,... | collective-permute-start | bytes 393224 | tf_op jit(solution)/shard_map/ppermute | solution.py:57
  214.2 18.4 %collective-permute-start.28 = (f32[4,2,32,128]{3,2,1,0:T(8,128)S(1)}, f32[4,2,32,128]{3,2,1,0:T(8,128)S(1)}, u32[]{:S(2)}, u32[]{:S(2)}) collective-permute-start(f32[4,2,32,128]{3,2,1,0:T(8,128)S(1)} %get-tuple-element.52), channel_id=1, source_target_pairs={{0,2},{1,3},{2,0},{3,1},{4,6},{5,7},{6,4},{7,5},{8,10},{9,11},{10,... | collective-permute-start | bytes 393224 | tf_op jit(solution)/shard_map/ppermute | solution.py:57
  217.2 15.5 %collective-permute-start.30 = (f32[4,2,32,128]{3,2,1,0:T(8,128)S(1)}, f32[4,2,32,128]{3,2,1,0:T(8,128)S(1)}, u32[]{:S(2)}, u32[]{:S(2)}) collective-permute-start(f32[4,2,32,128]{3,2,1,0:T(8,128)S(1)} %get-tuple-element.56), channel_id=1, source_target_pairs={{0,6},{1,7},{2,4},{3,5},{4,2},{5,3},{6,0},{7,1},{8,14},{9,15},{10,... | collective-permute-start | bytes 393224 | tf_op jit(solution)/shard_map/ppermute | solution.py:57
  218.1 19.6 %collective-permute-start.31 = (f32[4,2,32,128]{3,2,1,0:T(8,128)S(1)}, f32[4,2,32,128]{3,2,1,0:T(8,128)S(1)}, u32[]{:S(2)}, u32[]{:S(2)}) collective-permute-start(f32[4,2,32,128]{3,2,1,0:T(8,128)S(1)} %get-tuple-element.54), channel_id=1, source_target_pairs={{0,4},{1,5},{2,6},{3,7},{4,0},{5,1},{6,2},{7,3},{8,12},{9,13},{10,... | collective-permute-start | bytes 393224 | tf_op jit(solution)/shard_map/ppermute | solution.py:57
  220.0 17.6 %collective-permute-start.32 = (f32[4,2,32,128]{3,2,1,0:T(8,128)S(1)}, f32[4,2,32,128]{3,2,1,0:T(8,128)S(1)}, u32[]{:S(2)}, u32[]{:S(2)}) collective-permute-start(f32[4,2,32,128]{3,2,1,0:T(8,128)S(1)} %get-tuple-element.55), channel_id=1, source_target_pairs={{0,2},{1,3},{2,0},{3,1},{4,6},{5,7},{6,4},{7,5},{8,10},{9,11},{10,... | collective-permute-start | bytes 393224 | tf_op jit(solution)/shard_map/ppermute | solution.py:57

commit v2 on v1

v2 whole, which is shorter than its diff:
```python
import functools
import math

import jax
import jax.numpy as jnp
import ml_dtypes
import numpy as np
from jax import lax
from jax.experimental import pallas as pl
from jax.experimental.pallas import tpu as pltpu
from jax.sharding import PartitionSpec as P

power_floor = 0.1
f32 = jnp.float32
bf16 = jnp.bfloat16
nt_dims = (((1,), (1,)), ((), ()))
nn_dims = (((1,), (0,)), ((), ()))


def halves(table):
    high = table.astype(np.float32).astype(ml_dtypes.bfloat16)
    low = (table - high.astype(np.float64)).astype(ml_dtypes.bfloat16)
    return high, low


def window_table(length):
    index = np.arange(length)
    angles = 2.0 * math.pi / length * (index[:, None] * index[None, :] % length)
    window = 0.5 - 0.5 * np.cos(2.0 * math.pi / length * index)
    scale = window[None, :] / math.sqrt(length)
    high, low = halves(np.concatenate([np.cos(angles) * scale, np.sin(angles) * scale], 1))
    return high, low


def block_table(length, pieces):
    index = np.arange(length)
    angles = 2.0 * math.pi / length * (index[:, None] * index[None, :] % length)
    scale = 1.0 / math.sqrt(length)
    pair = [(t * scale).reshape(pieces, length // pieces, length) for t in (np.cos(angles), np.sin(angles))]
    return halves(np.concatenate(pair, 1).reshape(2 * length, length))


def split(value):
    high = value.astype(bf16)
    return high, (value - high.astype(f32)).astype(bf16)


def dot3(left, right, dims):
    lh, ll = left
    rh, rl = right
    dot = functools.partial(lax.dot_general, dimension_numbers=dims, preferred_element_type=f32)
    return dot(lh, rh) + dot(ll, rh) + dot(lh, rl)


def swap(block, axis, distance):
    size = lax.axis_size(axis)
    return lax.ppermute(block, axis, [(i, i ^ distance) for i in range(size)])


def demod_body(samples, table_high, table_low, *outs):
    table = (table_high[...], table_low[...])
    devices, half = outs[0].shape[:2]
    for s in range(samples.shape[1]):
        real = samples[0, s]
        imag = samples[1, s]
        upper = jnp.concatenate([real, imag], 1)
        lower = jnp.concatenate([imag, -real], 1)
        framed = jnp.concatenate([upper, lower], 0)
        result = dot3(table, split(framed), nt_dims)
        for device in range(devices):
            for side, out in enumerate(outs):
                start = (2 * device + side) * half
                out[device, :, s, :] = result[start:start + half]


def demodulate(samples, devices):
    _, sensors, blocks, channels = samples.shape
    step = min(8, sensors)
    half = channels // devices // 2
    high, low = window_table(channels)
    whole = pl.BlockSpec((channels, 2 * channels), lambda i: (0, 0))
    return pl.pallas_call(
        demod_body,
        grid=(sensors // step,),
        in_specs=[pl.BlockSpec((2, step, blocks, channels), lambda i: (0, i, 0, 0)), whole, whole],
        out_specs=[pl.BlockSpec((devices, half, step, 2 * blocks), lambda i: (0, 0, i, 0))] * 2,
        out_shape=[jax.ShapeDtypeStruct((devices, half, sensors, 2 * blocks), f32)] * 2,
        name="demod",
    )(samples, jnp.asarray(high), jnp.asarray(low))


def spectra_body(received, table_high, table_low, *refs, places):
    outs = refs[:-2]
    left_high, left_low = refs[-2:]
    sources, half, sensors, width = received.shape
    rows = half * sensors
    for p in range(sources):
        block = received[p].reshape(rows, width)
        turned = jnp.concatenate([block[:, width // 2:], -block[:, :width // 2]], 1)
        place = slice(p * width, (p + 1) * width)
        left_high[:rows, place], left_low[:rows, place] = split(block)
        left_high[rows:, place], left_low[rows:, place] = split(turned)
    total = dot3((left_high[...], left_low[...]), (table_high[...], table_low[...]), nn_dims)
    real = total[:rows]
    imag = total[rows:]
    scaling = lax.rsqrt(real * real + imag * imag + power_floor)
    for c, part in enumerate((real * scaling, imag * scaling)):
        part = part.reshape(half, sensors, part.shape[1])
        for t in range(part.shape[2] // 128):
            for out, place in zip(outs, places):
                out[:, t, c] = part[place, :, t * 128:(t + 1) * 128]


def whitened(received, pieces):
    sources, half, sensors, width = received.shape
    length = sources * width // 2
    rows = 2 * half * sensors
    high, low = block_table(length, sources)
    tiles = length // 128
    shapes = [jax.ShapeDtypeStruct((half, tiles, 2, sensors, 128), f32)]
    places = [slice(0, half)]
    for i in range(pieces):
        shapes.append(jax.ShapeDtypeStruct((half // pieces, tiles, 2, sensors, 128), f32))
        places.append(slice(i * half // pieces, (i + 1) * half // pieces))
    return pl.pallas_call(
        functools.partial(spectra_body, places=places),
        scratch_shapes=[pltpu.VMEM((rows, 2 * length), bf16)] * 2,
        out_shape=shapes,
        cost_estimate=pl.CostEstimate(
            flops=12 * rows * length * length, transcendentals=0, bytes_accessed=8 << 20
        ),
        name="spectra",
    )(received, jnp.asarray(high), jnp.asarray(low))


def gram_body(ids, bins, offsets, *refs, spans, parts, peers, devices, turns, turn, final, factor, group):
    window, refs = refs[:spans], refs[spans:]
    columns = [refs[parts * g:parts * (g + 1)] for g in range(peers)]
    refs = refs[parts * peers:]
    if final:
        before, refs = refs[0], refs[1:]
    outs, refs = (refs[:2], refs[2:]) if final else (refs[:1], refs[1:])
    extended, fresh, left_high, left_low, right_high, right_low, sums, plan, sems, fresh_sems = refs[:10]
    k = pl.program_id(0)
    steps = pl.num_programs(0)
    size = columns[0][0].shape[0]
    tiles, _, sensors, _ = window[0].shape[1:]
    rows = 2 * sensors
    alphas = sums.shape[0] // rows
    blocks = alphas // group
    starts = [sum(turns[:i]) for i in range(len(turns))]
    base = starts[turn] * devices

    def arrivals(chan, part):
        slot = lax.rem(chan, 2)
        return [
            pltpu.make_async_copy(columns[g][part].at[lax.rem(chan, size)], fresh.at[slot, g], fresh_sems.at[slot, g])
            for g in range(peers)
        ]

    def request(chan):
        for part in range(parts):

            @pl.when((chan >= part * size) & (chan < (part + 1) * size))
            def _():
                for copy in arrivals(chan, part):
                    copy.start()

    def pieces():
        copies = []
        start = 0
        for i, part in enumerate(window):
            copies.append(pltpu.make_async_copy(part, extended.at[start:start + part.shape[0]], sems.at[i]))
            start += part.shape[0]
        if final:
            copies.append(pltpu.make_async_copy(before.at[base:base + alphas], refs[10], sems.at[spans]))
        return copies

    @pl.when(k == 0)
    def _():
        request(k)
        for copy in pieces():
            copy.start()
        sums[...] = jnp.zeros(sums.shape, f32)

    for copy in arrivals(k, 0):
        copy.wait()
    request(k + 1)

    slot = lax.rem(k, 2)
    for g in range(peers):
        peer = jnp.bitwise_xor(ids[1], g)
        for c in range(2):
            place = pl.ds(pl.multiple_of((c * peers + peer) * sensors, sensors), sensors)
            for t in range(tiles):
                right_high[t, place], right_low[t, place] = split(fresh[slot, g, t, c])

    lane = lax.broadcasted_iota(jnp.int32, (rows, 128), 1)

    def build(chan, block, slot):
        for a in range(group):
            index = block * group + a
            source = chan + plan[0, index]
            tile = plan[1, index]
            rest = plan[2, index]
            turn = jnp.bitwise_and(128 - rest, 127)
            keep = lane < 128 - rest
            turned = []
            for t in range(tiles):
                data = extended[source, jnp.bitwise_and(tile + t, tiles - 1)].reshape(rows, 128)
                turned.append(pltpu.roll(data, turn, 1))
            for t in range(tiles):
                high, low = split(jnp.where(keep, turned[t], turned[(t + 1) % tiles]))
                left_high[slot, t, a * rows:(a + 1) * rows] = high
                left_low[slot, t, a * rows:(a + 1) * rows] = low

    def prepare(i, carry):
        position = base + i
        each, start = jnp.int32(turns[0]), jnp.int32(starts[0])
        for more, place in zip(turns[1:], starts[1:]):
            each = jnp.where(position < place * devices, each, more)
            start = jnp.where(position < place * devices, start, place)
        position = position - start * devices
        lane_group = position // each
        device = 2 * lax.rem(lane_group, devices // 2) + lane_group // (devices // 2)
        j = jnp.bitwise_xor(ids[0], device) * sum(turns) + start + lax.rem(position, each)
        q = bins[j]
        plan[0, i] = 2 * steps - offsets[j]
        plan[1, i] = lax.shift_right_logical(q, 7)
        plan[2, i] = jnp.bitwise_and(q, 127)
        return carry

    def joined(ref, extent):
        return jnp.concatenate([ref[t, :extent] for t in range(tiles)], 1)

    def multiply(block, slot):
        place = pl.ds(pl.multiple_of(block * (group * rows), group * rows), group * rows)
        left = (joined(left_high.at[slot], group * rows), joined(left_low.at[slot], group * rows))
        count = sums.shape[1]
        product = dot3(left, (joined(right_high, count), joined(right_low, count)), nt_dims)
        sums[place] = sums[place] + product

    @pl.when(k == 0)
    def _():
        lax.fori_loop(0, alphas, prepare, 0)
        for copy in pieces()[:spans]:
            copy.wait()
        build(0, 0, 0)

    def pair(i, carry):
        build(k, 2 * i + 1, 1)
        multiply(2 * i, 0)
        wrap = 2 * i + 2 == blocks
        build(jnp.where(wrap, jnp.minimum(k + 1, steps - 1), k), jnp.where(wrap, 0, 2 * i + 2), 0)
        multiply(2 * i + 1, 1)
        return carry

    lax.fori_loop(0, blocks // 2, pair, 0)

    @pl.when(k == steps - 1)
    def _():
        count = outs[0].shape[3]
        extent = outs[0].shape[0]
        if final:
            pieces()[spans].wait()

        for piece, out in enumerate(outs):

            def finish(j, carry):
                position = piece * extent + j
                cross = sums[pl.ds(pl.multiple_of(position * rows, rows), rows)]
                real = cross[:sensors, :count] + cross[sensors:, count:]
                imag = cross[sensors:, :count] - cross[:sensors, count:]
                if final:
                    real = (real + refs[10][position, 0]) * factor
                    imag = (imag + refs[10][position, 1]) * factor
                out[j, 0] = real
                out[j, 1] = imag
                return carry

            lax.fori_loop(0, extent, finish, 0, unroll=4)


def gram_sums(ids, bins, offsets, window, columns, before, turns, turn, devices, factor):
    half, tiles, _, sensors, _ = window[0].shape
    peers = len(columns)
    parts = len(columns[0])
    spans = len(window)
    final = before is not None
    outs = 2 if final else 1
    alphas = turns[turn] * devices if final else bins.shape[0]
    count = peers * sensors
    rows = 2 * sensors
    group = max(g for g in range(1, 1024 // rows + 1) if alphas % (2 * g) == 0)
    anywhere = pl.BlockSpec(memory_space=pl.ANY)
    shape = (alphas // outs, 2, sensors, count)
    return pl.pallas_call(
        functools.partial(
            gram_body, spans=spans, parts=parts, peers=peers, devices=devices, turns=turns, turn=turn, final=final, factor=factor, group=group
        ),
        grid_spec=pltpu.PrefetchScalarGridSpec(
            num_scalar_prefetch=3,
            grid=(half,),
            in_specs=[anywhere] * (spans + parts * peers + outs - 1),
            out_specs=[pl.BlockSpec(shape, lambda k, *_: (0, 0, 0, 0))] * outs,
            scratch_shapes=[
                pltpu.VMEM((3 * half, tiles, 2, sensors, 128), f32),
                pltpu.VMEM((2, peers, tiles, 2, sensors, 128), f32),
                pltpu.VMEM((2, tiles, group * rows + 16, 128), bf16),
                pltpu.VMEM((2, tiles, group * rows + 16, 128), bf16),
                pltpu.VMEM((tiles, 2 * count + 16, 128), bf16),
                pltpu.VMEM((tiles, 2 * count + 16, 128), bf16),
                pltpu.VMEM((alphas * rows, 2 * count), f32),
                pltpu.SMEM((3, alphas), jnp.int32),
                pltpu.SemaphoreType.DMA((spans + 1,)),
                pltpu.SemaphoreType.DMA((2, peers)),
            ]
            + [pltpu.VMEM((alphas, 2, sensors, count), f32)] * (outs - 1),
        ),
        out_shape=[jax.ShapeDtypeStruct(shape, f32)] * outs,
        cost_estimate=pl.CostEstimate(
            flops=6 * half * tiles * 128 * alphas * rows * 2 * count, transcendentals=0, bytes_accessed=8 << 20
        ),
        name="gram",
    )(ids, bins, offsets, *window, *[part for group in columns for part in group], *([before] if final else []))


def on_device(samples, bins, offsets):
    chan_count = lax.axis_size("chan")
    peers = lax.axis_size("sensor")
    channels = samples.shape[3]
    ids = jnp.stack([lax.axis_index("chan"), lax.axis_index("sensor")]).astype(jnp.int32)
    pieces = demodulate(samples, chan_count)
    received = []
    for side in range(2):
        received.append(lax.all_to_all(pieces[side], "chan", split_axis=0, concat_axis=0, tiled=True))
    route = [(i, (i + 1) % chan_count) for i in range(chan_count)]
    upper_whole, *uppers = whitened(received[1], 2)
    upper_rim = lax.ppermute(upper_whole, "chan", route)
    columns = [{0: part} for part in uppers]
    single = [r for r in range(1, peers) if r & (r - 1) == 0]
    for i, gathered in enumerate(columns):
        for r in single if i else single[::-1]:
            gathered[r] = swap(gathered[0], "sensor", r)
    for i, gathered in enumerate(columns):
        for r in range(1, peers):
            if r not in single:
                bits = [b for b in single if r & b]
                bit = bits[0] if i else bits[-1]
                gathered[r] = swap(gathered[r ^ bit], "sensor", bit)
    upper_columns = [[gathered[r] for gathered in columns] for r in range(peers)]
    (lower,) = whitened(received[0], 0)
    lower_columns = [[lower]] + [[swap(lower, "sensor", r)] for r in range(1, peers)]
    lower_rim = lax.ppermute(lower, "chan", route)
    factor = 1.0 / math.sqrt(channels * samples.shape[2] * chan_count)
    share = bins.shape[0] // chan_count
    turns = (share - share // 4, share // 4)
    upper_window = [upper_rim, lower] + uppers
    lower_window = [lower_rim, upper_rim, lower]
    scan = functools.partial(gram_sums, ids, bins, offsets, devices=chan_count, factor=factor)
    upper = scan(upper_window, upper_columns, None, turns, 0)[0]
    results = []
    for side in range(2):
        same, other = scan(lower_window, lower_columns, upper, turns, side)
        near = swap(other, "chan", 1)
        each = same.shape[0] // (chan_count // 2)
        total = None
        for q in range(chan_count // 2 - 1, -1, -1):
            place = slice(q * each, (q + 1) * each)
            both = same[place] + near[place]
            if q:
                both = swap(both, "chan", 2 * q)
            total = both if total is None else total + both
        results.append(total)
    return jnp.concatenate(results, 0)


def solution(mesh):
    return jax.shard_map(
        on_device,
        mesh=mesh,
        in_specs=(P(None, "sensor", "chan", None), P(), P()),
        out_specs=P("chan", None, "sensor", None),
        check_vma=False,
    )
```

time: 240 us -> 228 us (0.950)
  waiting for transfers between devices: 80.3 us -> 42.3 us
  blocking collectives: 0 us -> 33 us
  Pallas kernels: 112 us -> 103 us
  starting transfers between devices: 40.5 us -> 43.2 us
    ppermute x31 -> x17, waiting for transfers between devices: 80.3 us -> 28.5 us  [swap(): return lax.ppermute(block, axis, [(i, i ^ distance) for i in range(size)])]
    all_to_all x0 -> x1, blocking collectives: none -> 33 us  [on_device(): lax.all_to_all(pieces[side], 'chan', split_axis=0, concat_axis=0, tiled=T...]
    all_to_all x0 -> x1, waiting for transfers between devices: none -> 13.8 us  [on_device(): lax.all_to_all(pieces[side], 'chan', split_axis=0, concat_axis=0, tiled=T...]
    pallas_call x3, Pallas kernels: 94.3 us -> 87.4 us  [gram_sums(): pl.pallas_call(functools.partial(gram_body, spans=spans, parts=parts, pee...]
    all_to_all x0 -> x1, starting transfers between devices: none -> 3.56 us  [on_device(): lax.all_to_all(pieces[side], 'chan', split_axis=0, concat_axis=0, tiled=T...]
    ppermute x31 -> x17, starting transfers between devices: 40.5 us -> 39.6 us  [swap(): return lax.ppermute(block, axis, [(i, i ^ distance) for i in range(size)])]
  transfers between devices with their start and end apart: 33 -> 20, of which waited for: 12 -> 8; matrix products, arithmetic and copies ran while one was open for 1% -> 1% of each run, Pallas kernels for 34% -> 29%
where the time goes in v2:
time: 228 us; the launch traced here: 226 us
  Pallas kernels  103 us (45%)
  starting transfers between devices  43.2 us (19%)
  waiting for transfers between devices  42.3 us (19%)
  blocking collectives  33 us (14%)
  other arithmetic  3.36 us (1%)
    pallas_call x3, Pallas kernels, gram_sums(): pl.pallas_call(functools.partial(gram_body, spans=spans, parts=parts, pee...  87.4 us
    ppermute x17, starting transfers between devices, swap(): return lax.ppermute(block, axis, [(i, i ^ distance) for i in range(size)])  39.6 us
    all_to_all x1, blocking collectives, on_device(): lax.all_to_all(pieces[side], 'chan', split_axis=0, concat_axis=0, tiled=T...  33 us
    ppermute x17, waiting for transfers between devices, swap(): return lax.ppermute(block, axis, [(i, i ^ distance) for i in range(size)])  28.5 us
    all_to_all x1, waiting for transfers between devices, on_device(): lax.all_to_all(pieces[side], 'chan', split_axis=0, concat_axis=0, tiled=T...  13.8 us
    pallas_call x2, Pallas kernels, whitened(): pl.pallas_call(functools.partial(spectra_body, places=places), scratch_sh...  10 us
    pallas_call x1, Pallas kernels, demodulate(): pl.pallas_call(demod_body, grid=(sensors // step,), in_specs=[pl.BlockSpe...  5.15 us
  transfers between devices with their start and end apart: 20, of which 8 were waited for; matrix products, arithmetic and copies ran while one was open for 1% of the time, Pallas kernels for 29%

profile of v2, /device:TPU:0, one launch (start us, length us, event | category | flops | bytes accessed | tf_op | source)
XLA Modules:
  0.0 226.4 jit_solution(11699176810318409987)
XLA Ops:
  0.0 5.1 %demod.1 = (f32[8,8,32,128]{3,2,1,0:T(8,128)}, f32[8,8,32,128]{3,2,1,0:T(8,128)}) custom-call(f32[2,32,64,128]{3,2,1,0:T(8,128)} %samples.1, bf16[128,256]{1,0:T(8,128)(2,1)} %constant.16.clone.table_high, bf16[128,256]{1,0:T(8,128)(2,1)} %constant.17.clone.table_low), custom_call_target="tpu_custom_call" | custom-call | tf_op jit(solution)/shard_map/demod/pallas_call | solution.py:82
  5.2 33.0 %all_to_all.10.received = f32[8,8,32,128]{3,2,1,0:T(8,128)} all-to-all(f32[8,8,32,128]{3,2,1,0:T(8,128)} %get-tuple-element.15), channel_id=1, replica_groups=mesh['sensor'=4,'chan'=8] {'chan'}, dimensions={0} | all-to-all | bytes 2097152 | tf_op jit(solution)/shard_map/all_to_all | solution.py:336
  38.2 3.6 %all-to-all-start = ((f32[8,8,32,128]{3,2,1,0:T(8,128)}), f32[8,8,32,128]{3,2,1,0:T(8,128)S(1)}, u32[]{:S(2)}, u32[]{:S(2)}) async-start(f32[8,8,32,128]{3,2,1,0:T(8,128)} %get-tuple-element.14), calls=%async_computation | async-start | bytes 2097152 | tf_op jit(solution)/shard_map/all_to_all | solution.py:336
  41.7 5.2 %spectra.3 = (f32[8,4,2,32,128]{4,3,2,1,0:T(8,128)}, f32[4,4,2,32,128]{4,3,2,1,0:T(8,128)}, f32[4,4,2,32,128]{4,3,2,1,0:T(8,128)}) custom-call(f32[8,8,32,128]{3,2,1,0:T(8,128)} %all_to_all.10.received, bf16[1024,512]{1,0:T(8,128)(2,1)} %constant.18.clone.table_high, bf16[1024,512]{1,0:T(8,128)(2,1)} %constant.19.clone.table_low), custom_call_target="tpu_custom_call" | custom-call | flops 1610612736 | bytes 8388608 | tf_op jit(solution)/shard_map/spectra/pallas_call | solution.py:125
  47.0 1.5 collective-permute-start.5
  48.5 1.5 collective-permute-start.8
  50.0 0.0 collective-permute-start.1
  50.0 0.5 collective-permute-start.7
  50.5 0.5 collective-permute-start.6
  51.0 11.0 %collective-permute-done.5.refs_6_ = f32[4,4,2,32,128]{4,3,2,1,0:T(8,128)S(1)} collective-permute-done((f32[4,4,2,32,128]{4,3,2,1,0:T(8,128)}, f32[4,4,2,32,128]{4,3,2,1,0:T(8,128)S(1)}, u32[]{:S(2)}, u32[]{:S(2)}) %collective-permute-start.5) | collective-permute-done | bytes 524320 | tf_op jit(solution)/shard_map/ppermute | solution.py:57
  62.0 0.0 copy-start.4
  62.0 1.5 collective-permute-start.9
  63.5 0.1 collective-permute-done.8.refs_9_
  63.6 1.4 collective-permute-start.10
  65.0 0.7 pad_add_fusion.ids
  65.6 13.8 %all-to-all-done.received = f32[8,8,32,128]{3,2,1,0:T(8,128)S(1)} async-done(((f32[8,8,32,128]{3,2,1,0:T(8,128)}), f32[8,8,32,128]{3,2,1,0:T(8,128)S(1)}, u32[]{:S(2)}, u32[]{:S(2)}) %all-to-all-start) | async-done | bytes 1048608 | tf_op jit(solution)/shard_map/all_to_all | solution.py:336
  79.5 0.0 copy-start
  79.5 1.0 copy-done
  80.4 4.8 %spectra.2.refs_1_.refs_2_.refs_3_ = f32[8,4,2,32,128]{4,3,2,1,0:T(8,128)} custom-call(f32[8,8,32,128]{3,2,1,0:T(8,128)} %copy-done, bf16[1024,512]{1,0:T(8,128)(2,1)} %constant.18.clone.table_high, bf16[1024,512]{1,0:T(8,128)(2,1)} %constant.19.clone.table_low), custom_call_target="tpu_custom_call" | custom-call | flops 1610612736 | bytes 8388608 | tf_op jit(solution)/shard_map/spectra/pallas_call | solution.py:125
  85.2 0.0 collective-permute-done.7.refs_8_
  85.2 2.4 %collective-permute-start.4 = (f32[8,4,2,32,128]{4,3,2,1,0:T(8,128)}, f32[8,4,2,32,128]{4,3,2,1,0:T(8,128)S(1)}, u32[]{:S(2)}, u32[]{:S(2)}) collective-permute-start(f32[8,4,2,32,128]{4,3,2,1,0:T(8,128)} %spectra.2.refs_1_.refs_2_.refs_3_), channel_id=1, source_target_pairs={{0,24},{8,16},{16,8},{24,0},{1,25},{9,17},{17,9},{25,1},{2,26},{10... | collective-permute-start | bytes 3145736 | tf_op jit(solution)/shard_map/ppermute | solution.py:57
  87.7 0.0 collective-permute-done.6.refs_7_
  87.7 0.5 collective-permute-start.3
  88.2 0.0 collective-permute-done.9.refs_10_
  88.2 0.5 collective-permute-start.2
  88.7 0.0 collective-permute-done.10.refs_11_
  88.7 0.0 collective-permute-start
  88.7 0.0 collective-permute-done.1.refs_0_.refs_1_
  88.7 0.0 copy-done.4
  88.7 0.0 copy-start.2
  88.8 1.0 copy-done.2
  89.7 40.4 %gram.3.refs_7_ = f32[64,2,32,128]{3,2,1,0:T(8,128)} custom-call(s32[2]{0:T(128)} %pad_add_fusion.ids, s32[64]{0:T(128)} %bins.5, s32[64]{0:T(128)} %offsets.5, f32[8,4,2,32,128]{4,3,2,1,0:T(8,128)} %copy-done.2, f32[8,4,2,32,128]{4,3,2,1,0:T(8,128)} %spectra.2.refs_1_.refs_2_.refs_3_, f32[4,4,2,32,128]{4,3,2,1,0:T(8,128)} %get-tuple-element.17.refs_2_.refs_4_, ...), custom_call_target="tpu_custom_call" | custom-call | flops 25769803776 | bytes 8388608 | tf_op jit(solution)/shard_map/gram/pallas_call | solution.py:297
  130.1 0.0 collective-permute-done.4.refs_6_
  130.1 0.0 copy-start.3
  130.2 3.4 %collective-permute-done.3.refs_5_ = f32[8,4,2,32,128]{4,3,2,1,0:T(8,128)} collective-permute-done((f32[8,4,2,32,128]{4,3,2,1,0:T(8,128)}, f32[8,4,2,32,128]{4,3,2,1,0:T(8,128)}, u32[]{:S(2)}, u32[]{:S(2)}) %collective-permute-start.3) | collective-permute-done | bytes 1048608 | tf_op jit(solution)/shard_map/ppermute | solution.py:57
  133.5 0.1 collective-permute-done.2.refs_4_
  133.6 0.0 collective-permute-done.refs_0_
  133.6 0.0 copy-done.3
  133.6 32.7 %gram.4 = (f32[24,2,32,128]{3,2,1,0:T(8,128)}, f32[24,2,32,128]{3,2,1,0:T(8,128)}) custom-call(s32[2]{0:T(128)} %pad_add_fusion.ids, s32[64]{0:T(128)} %bins.5, s32[64]{0:T(128)} %offsets.5, f32[8,4,2,32,128]{4,3,2,1,0:T(8,128)} %collective-permute-done.refs_0_, f32[8,4,2,32,128]{4,3,2,1,0:T(8,128)} %copy-done.2, ...), custom_call_target="tpu_custom_call" | custom-call | flops 19327352832 | bytes 8388608 | tf_op jit(solution)/shard_map/gram/pallas_call | solution.py:297
  166.3 0.0 copy-start.1
  166.3 20.0 %collective-permute-start.11 = (f32[24,2,32,128]{3,2,1,0:T(8,128)}, f32[24,2,32,128]{3,2,1,0:T(8,128)S(1)}, u32[]{:S(2)}, u32[]{:S(2)}) collective-permute-start(f32[24,2,32,128]{3,2,1,0:T(8,128)} %get-tuple-element.20), channel_id=1, source_target_pairs={{0,1},{1,0},{2,3},{3,2},{4,5},{5,4},{6,7},{7,6},{8,9},{9,8},{10,11... | collective-permute-start | bytes 2359304 | tf_op jit(solution)/shard_map/ppermute | solution.py:57
  186.3 14.3 %gram.5 = (f32[8,2,32,128]{3,2,1,0:T(8,128)}, f32[8,2,32,128]{3,2,1,0:T(8,128)}) custom-call(s32[2]{0:T(128)} %pad_add_fusion.ids, s32[64]{0:T(128)} %bins.5, s32[64]{0:T(128)} %offsets.5, f32[8,4,2,32,128]{4,3,2,1,0:T(8,128)} %collective-permute-done.refs_0_, f32[8,4,2,32,128]{4,3,2,1,0:T(8,128)} %copy-done.2, ...), custom_call_target="tpu_custom_call" | custom-call | flops 6442450944 | bytes 8388608 | tf_op jit(solution)/shard_map/gram/pallas_call | solution.py:297
  200.6 0.2 collective-permute-start.15
  200.8 1.6 collective-permute-done.15
  202.4 0.9 slice_add_fusion.6
  203.4 2.5 %collective-permute-start.17 = (f32[2,2,32,128]{3,2,1,0:T(8,128)S(1)}, f32[2,2,32,128]{3,2,1,0:T(8,128)S(1)}, u32[]{:S(2)}, u32[]{:S(2)}) collective-permute-start(f32[2,2,32,128]{3,2,1,0:T(8,128)S(1)} %get-tuple-element.26), channel_id=1, source_target_pairs={{0,4},{1,5},{2,6},{3,7},{4,0},{5,1},{6,2},{7,3},{8,12},{9,13},{10,... | collective-permute-start | bytes 196616 | tf_op jit(solution)/shard_map/ppermute | solution.py:57
  205.8 0.0 collective-permute-start.18
  205.9 1.9 collective-permute-start.16
  207.8 0.0 collective-permute-done.11
  207.8 0.0 copy-done.1
  207.8 0.1 slice_add_fusion.2
  207.9 1.6 collective-permute-start.13
  209.5 0.9 collective-permute-start.14
  210.4 0.0 collective-permute-done.17
  210.4 1.9 collective-permute-start.12
  212.4 0.0 collective-permute-done.18
  212.4 0.3 collective-permute-done.16
  212.7 0.9 fusion.1
  213.5 12.1 %collective-permute-done.13 = f32[6,2,32,128]{3,2,1,0:T(8,128)S(1)} collective-permute-done((f32[6,2,32,128]{3,2,1,0:T(8,128)S(1)}, f32[6,2,32,128]{3,2,1,0:T(8,128)S(1)}, u32[]{:S(2)}, u32[]{:S(2)}) %collective-permute-start.13) | collective-permute-done | bytes 196640 | tf_op jit(solution)/shard_map/ppermute | solution.py:57
  225.6 0.0 collective-permute-done.14
  225.6 0.0 collective-permute-done.12
  225.6 0.1 fusion
  225.7 0.7 pad_maximum_fusion
Async XLA Ops:
  38.2 41.3 %all-to-all-start = ((f32[8,8,32,128]{3,2,1,0:T(8,128)}), f32[8,8,32,128]{3,2,1,0:T(8,128)S(1)}, u32[]{:S(2)}, u32[]{:S(2)}) async-start(f32[8,8,32,128]{3,2,1,0:T(8,128)} %get-tuple-element.14), calls=%async_computation | async-start | bytes 2097152 | tf_op jit(solution)/shard_map/all_to_all | solution.py:336
  47.0 15.0 %collective-permute-start.5 = (f32[4,4,2,32,128]{4,3,2,1,0:T(8,128)}, f32[4,4,2,32,128]{4,3,2,1,0:T(8,128)S(1)}, u32[]{:S(2)}, u32[]{:S(2)}) collective-permute-start(f32[4,4,2,32,128]{4,3,2,1,0:T(8,128)} %get-tuple-element.17.refs_2_.refs_4_), channel_id=1, source_target_pairs={{0,8},{8,0},{16,24},{24,16},{1,9},{9,1},{17,25},{25,17},{2,10},{10... | collective-permute-start | bytes 1572872 | tf_op jit(solution)/shard_map/ppermute | solution.py:57
  48.5 15.1 %collective-permute-start.8 = (f32[4,4,2,32,128]{4,3,2,1,0:T(8,128)}, f32[4,4,2,32,128]{4,3,2,1,0:T(8,128)}, u32[]{:S(2)}, u32[]{:S(2)}) collective-permute-start(f32[4,4,2,32,128]{4,3,2,1,0:T(8,128)} %get-tuple-element.18.refs_3_.refs_5_), channel_id=1, source_target_pairs={{0,16},{8,24},{16,0},{24,8},{1,17},{9,25},{17,1},{25,9},{2,18},{10... | collective-permute-start | bytes 1572872 | tf_op jit(solution)/shard_map/ppermute | solution.py:57
  50.0 38.8 %collective-permute-start.1 = (f32[8,4,2,32,128]{4,3,2,1,0:T(8,128)}, f32[8,4,2,32,128]{4,3,2,1,0:T(8,128)S(1)}, u32[]{:S(2)}, u32[]{:S(2)}) collective-permute-start(f32[8,4,2,32,128]{4,3,2,1,0:T(8,128)} %get-tuple-element.16), channel_id=1, source_target_pairs={{0,1},{1,2},{2,3},{3,4},{4,5},{5,6},{6,7},{7,0},{8,9},{9,10},{10,1... | collective-permute-start | bytes 3145736 | tf_op jit(solution)/shard_map/ppermute | solution.py:339
  50.0 35.3 %collective-permute-start.7 = (f32[4,4,2,32,128]{4,3,2,1,0:T(8,128)}, f32[4,4,2,32,128]{4,3,2,1,0:T(8,128)}, u32[]{:S(2)}, u32[]{:S(2)}) collective-permute-start(f32[4,4,2,32,128]{4,3,2,1,0:T(8,128)} %get-tuple-element.17.refs_2_.refs_4_), channel_id=1, source_target_pairs={{0,16},{8,24},{16,0},{24,8},{1,17},{9,25},{17,1},{25,9},{2,18},{10... | collective-permute-start | bytes 1572872 | tf_op jit(solution)/shard_map/ppermute | solution.py:57
  50.5 37.2 %collective-permute-start.6 = (f32[4,4,2,32,128]{4,3,2,1,0:T(8,128)}, f32[4,4,2,32,128]{4,3,2,1,0:T(8,128)}, u32[]{:S(2)}, u32[]{:S(2)}) collective-permute-start(f32[4,4,2,32,128]{4,3,2,1,0:T(8,128)} %get-tuple-element.18.refs_3_.refs_5_), channel_id=1, source_target_pairs={{0,8},{8,0},{16,24},{24,16},{1,9},{9,1},{17,25},{25,17},{2,10},{10... | collective-permute-start | bytes 1572872 | tf_op jit(solution)/shard_map/ppermute | solution.py:57
  62.0 26.8 %copy-start.4 = (f32[4,4,2,32,128]{4,3,2,1,0:T(8,128)}, f32[4,4,2,32,128]{4,3,2,1,0:T(8,128)S(1)}, u32[]{:S(2)}) copy-start(f32[4,4,2,32,128]{4,3,2,1,0:T(8,128)S(1)} %collective-permute-done.5.refs_6_) | copy-start | bytes 1572868
  62.0 26.2 %collective-permute-start.9 = (f32[4,4,2,32,128]{4,3,2,1,0:T(8,128)S(1)}, f32[4,4,2,32,128]{4,3,2,1,0:T(8,128)}, u32[]{:S(2)}, u32[]{:S(2)}) collective-permute-start(f32[4,4,2,32,128]{4,3,2,1,0:T(8,128)S(1)} %collective-permute-done.5.refs_6_), channel_id=1, source_target_pairs={{0,16},{8,24},{16,0},{24,8},{1,17},{9,25},{17,1},{25,9},{2,18},{10... | collective-permute-start | bytes 1572872 | tf_op jit(solution)/shard_map/ppermute | solution.py:57
  63.6 25.2 %collective-permute-start.10 = (f32[4,4,2,32,128]{4,3,2,1,0:T(8,128)}, f32[4,4,2,32,128]{4,3,2,1,0:T(8,128)}, u32[]{:S(2)}, u32[]{:S(2)}) collective-permute-start(f32[4,4,2,32,128]{4,3,2,1,0:T(8,128)} %collective-permute-done.8.refs_9_), channel_id=1, source_target_pairs={{0,8},{8,0},{16,24},{24,16},{1,9},{9,1},{17,25},{25,17},{2,10},{10... | collective-permute-start | bytes 1572872 | tf_op jit(solution)/shard_map/ppermute | solution.py:57
  79.5 1.0 copy-start
  85.2 44.9 %collective-permute-start.4 = (f32[8,4,2,32,128]{4,3,2,1,0:T(8,128)}, f32[8,4,2,32,128]{4,3,2,1,0:T(8,128)S(1)}, u32[]{:S(2)}, u32[]{:S(2)}) collective-permute-start(f32[8,4,2,32,128]{4,3,2,1,0:T(8,128)} %spectra.2.refs_1_.refs_2_.refs_3_), channel_id=1, source_target_pairs={{0,24},{8,16},{16,8},{24,0},{1,25},{9,17},{17,9},{25,1},{2,26},{10... | collective-permute-start | bytes 3145736 | tf_op jit(solution)/shard_map/ppermute | solution.py:57
  87.7 45.9 %collective-permute-start.3 = (f32[8,4,2,32,128]{4,3,2,1,0:T(8,128)}, f32[8,4,2,32,128]{4,3,2,1,0:T(8,128)}, u32[]{:S(2)}, u32[]{:S(2)}) collective-permute-start(f32[8,4,2,32,128]{4,3,2,1,0:T(8,128)} %spectra.2.refs_1_.refs_2_.refs_3_), channel_id=1, source_target_pairs={{0,16},{8,24},{16,0},{24,8},{1,17},{9,25},{17,1},{25,9},{2,18},{10... | collective-permute-start | bytes 3145736 | tf_op jit(solution)/shard_map/ppermute | solution.py:57
  88.2 45.4 %collective-permute-start.2 = (f32[8,4,2,32,128]{4,3,2,1,0:T(8,128)}, f32[8,4,2,32,128]{4,3,2,1,0:T(8,128)}, u32[]{:S(2)}, u32[]{:S(2)}) collective-permute-start(f32[8,4,2,32,128]{4,3,2,1,0:T(8,128)} %spectra.2.refs_1_.refs_2_.refs_3_), channel_id=1, source_target_pairs={{0,8},{8,0},{16,24},{24,16},{1,9},{9,1},{17,25},{25,17},{2,10},{10... | collective-permute-start | bytes 3145736 | tf_op jit(solution)/shard_map/ppermute | solution.py:57
  88.7 44.9 %collective-permute-start = (f32[8,4,2,32,128]{4,3,2,1,0:T(8,128)}, f32[8,4,2,32,128]{4,3,2,1,0:T(8,128)}, u32[]{:S(2)}, u32[]{:S(2)}) collective-permute-start(f32[8,4,2,32,128]{4,3,2,1,0:T(8,128)} %spectra.2.refs_1_.refs_2_.refs_3_), channel_id=1, source_target_pairs={{0,1},{1,2},{2,3},{3,4},{4,5},{5,6},{6,7},{7,0},{8,9},{9,10},{10,1... | collective-permute-start | bytes 3145736 | tf_op jit(solution)/shard_map/ppermute | solution.py:354
  88.7 1.0 copy-start.2
  130.1 3.5 %copy-start.3 = (f32[8,4,2,32,128]{4,3,2,1,0:T(8,128)}, f32[8,4,2,32,128]{4,3,2,1,0:T(8,128)S(1)}, u32[]{:S(2)}) copy-start(f32[8,4,2,32,128]{4,3,2,1,0:T(8,128)S(1)} %collective-permute-done.4.refs_6_) | copy-start | bytes 3145732
  166.3 41.5 %copy-start.1 = (f32[24,2,32,128]{3,2,1,0:T(8,128)S(1)}, f32[24,2,32,128]{3,2,1,0:T(8,128)}, u32[]{:S(2)}) copy-start(f32[24,2,32,128]{3,2,1,0:T(8,128)} %get-tuple-element.19) | copy-start | bytes 2359300
  166.3 41.5 %collective-permute-start.11 = (f32[24,2,32,128]{3,2,1,0:T(8,128)}, f32[24,2,32,128]{3,2,1,0:T(8,128)S(1)}, u32[]{:S(2)}, u32[]{:S(2)}) collective-permute-start(f32[24,2,32,128]{3,2,1,0:T(8,128)} %get-tuple-element.20), channel_id=1, source_target_pairs={{0,1},{1,0},{2,3},{3,2},{4,5},{5,4},{6,7},{7,6},{8,9},{9,8},{10,11... | collective-permute-start | bytes 2359304 | tf_op jit(solution)/shard_map/ppermute | solution.py:57
  200.6 1.8 collective-permute-start.15
  203.4 7.1 %collective-permute-start.17 = (f32[2,2,32,128]{3,2,1,0:T(8,128)S(1)}, f32[2,2,32,128]{3,2,1,0:T(8,128)S(1)}, u32[]{:S(2)}, u32[]{:S(2)}) collective-permute-start(f32[2,2,32,128]{3,2,1,0:T(8,128)S(1)} %get-tuple-element.26), channel_id=1, source_target_pairs={{0,4},{1,5},{2,6},{3,7},{4,0},{5,1},{6,2},{7,3},{8,12},{9,13},{10,... | collective-permute-start | bytes 196616 | tf_op jit(solution)/shard_map/ppermute | solution.py:57
  205.8 6.6 %collective-permute-start.18 = (f32[2,2,32,128]{3,2,1,0:T(8,128)S(1)}, f32[2,2,32,128]{3,2,1,0:T(8,128)S(1)}, u32[]{:S(2)}, u32[]{:S(2)}) collective-permute-start(f32[2,2,32,128]{3,2,1,0:T(8,128)S(1)} %get-tuple-element.27), channel_id=1, source_target_pairs={{0,2},{1,3},{2,0},{3,1},{4,6},{5,7},{6,4},{7,5},{8,10},{9,11},{10,... | collective-permute-start | bytes 196616 | tf_op jit(solution)/shard_map/ppermute | solution.py:57
  205.9 6.8 %collective-permute-start.16 = (f32[2,2,32,128]{3,2,1,0:T(8,128)S(1)}, f32[2,2,32,128]{3,2,1,0:T(8,128)S(1)}, u32[]{:S(2)}, u32[]{:S(2)}) collective-permute-start(f32[2,2,32,128]{3,2,1,0:T(8,128)S(1)} %get-tuple-element.28), channel_id=1, source_target_pairs={{0,6},{1,7},{2,4},{3,5},{4,2},{5,3},{6,0},{7,1},{8,14},{9,15},{10,... | collective-permute-start | bytes 196616 | tf_op jit(solution)/shard_map/ppermute | solution.py:57
  207.9 17.7 %collective-permute-start.13 = (f32[6,2,32,128]{3,2,1,0:T(8,128)S(1)}, f32[6,2,32,128]{3,2,1,0:T(8,128)S(1)}, u32[]{:S(2)}, u32[]{:S(2)}) collective-permute-start(f32[6,2,32,128]{3,2,1,0:T(8,128)S(1)} %get-tuple-element.23), channel_id=1, source_target_pairs={{0,4},{1,5},{2,6},{3,7},{4,0},{5,1},{6,2},{7,3},{8,12},{9,13},{10,... | collective-permute-start | bytes 589832 | tf_op jit(solution)/shard_map/ppermute | solution.py:57
  209.5 16.1 %collective-permute-start.14 = (f32[6,2,32,128]{3,2,1,0:T(8,128)S(1)}, f32[6,2,32,128]{3,2,1,0:T(8,128)S(1)}, u32[]{:S(2)}, u32[]{:S(2)}) collective-permute-start(f32[6,2,32,128]{3,2,1,0:T(8,128)S(1)} %get-tuple-element.24), channel_id=1, source_target_pairs={{0,2},{1,3},{2,0},{3,1},{4,6},{5,7},{6,4},{7,5},{8,10},{9,11},{10,... | collective-permute-start | bytes 589832 | tf_op jit(solution)/shard_map/ppermute | solution.py:57
  210.4 15.2 %collective-permute-start.12 = (f32[6,2,32,128]{3,2,1,0:T(8,128)S(1)}, f32[6,2,32,128]{3,2,1,0:T(8,128)S(1)}, u32[]{:S(2)}, u32[]{:S(2)}) collective-permute-start(f32[6,2,32,128]{3,2,1,0:T(8,128)S(1)} %get-tuple-element.25), channel_id=1, source_target_pairs={{0,6},{1,7},{2,4},{3,5},{4,2},{5,3},{6,0},{7,1},{8,14},{9,15},{10,... | collective-permute-start | bytes 589832 | tf_op jit(solution)/shard_map/ppermute | solution.py:57

commit v3 on v2

--- a/solution.py
+++ b/solution.py
@@ -90,8 +90,8 @@
 
 
 def spectra_body(received, table_high, table_low, *refs, places):
-    outs = refs[:-2]
-    left_high, left_low = refs[-2:]
+    outs = refs[:-3]
+    left_high, left_low, sums = refs[-3:]
     sources, half, sensors, width = received.shape
     rows = half * sensors
     for p in range(sources):
@@ -100,15 +100,23 @@
         place = slice(p * width, (p + 1) * width)
         left_high[:rows, place], left_low[:rows, place] = split(block)
         left_high[rows:, place], left_low[rows:, place] = split(turned)
-    total = dot3((left_high[...], left_low[...]), (table_high[...], table_low[...]), nn_dims)
-    real = total[:rows]
-    imag = total[rows:]
-    scaling = lax.rsqrt(real * real + imag * imag + power_floor)
-    for c, part in enumerate((real * scaling, imag * scaling)):
-        part = part.reshape(half, sensors, part.shape[1])
-        for t in range(part.shape[2] // 128):
-            for out, place in zip(outs, places):
-                out[:, t, c] = part[place, :, t * 128:(t + 1) * 128]
+    product = dot3((left_high[...], left_low[...]), (table_high[...], table_low[...]), nn_dims)
+
+    @pl.when(pl.program_id(0) == 0)
+    def _():
+        sums[...] = product
+
+    @pl.when(pl.program_id(0) == 1)
+    def _():
+        total = sums[...] + product
+        real = total[:rows]
+        imag = total[rows:]
+        scaling = lax.rsqrt(real * real + imag * imag + power_floor)
+        for c, part in enumerate((real * scaling, imag * scaling)):
+            part = part.reshape(half, sensors, part.shape[1])
+            for t in range(part.shape[2] // 128):
+                for out, place in zip(outs, places):
+                    out[:, t, c] = part[place, :, t * 128:(t + 1) * 128]
 
 
 def whitened(received, pieces):
@@ -124,7 +132,11 @@
         places.append(slice(i * half // pieces, (i + 1) * half // pieces))
     return pl.pallas_call(
         functools.partial(spectra_body, places=places),
-        scratch_shapes=[pltpu.VMEM((rows, 2 * length), bf16)] * 2,
+        grid=(2,),
+        in_specs=[pl.BlockSpec((sources // 2, half, sensors, width), lambda i: (i, 0, 0, 0))]
+        + [pl.BlockSpec((length, length), lambda i: (i, 0))] * 2,
+        out_specs=[pl.BlockSpec(shape.shape, lambda i: (0, 0, 0, 0, 0)) for shape in shapes],
+        scratch_shapes=[pltpu.VMEM((rows, length), bf16)] * 2 + [pltpu.VMEM((rows, length), f32)],
         out_shape=shapes,
         cost_estimate=pl.CostEstimate(
             flops=12 * rows * length * length, transcendentals=0, bytes_accessed=8 << 20

time: 228 us -> 228 us (level)
  no operation moved by 1% of the time
where the time goes in v3:
time: 228 us; the launch traced here: 226 us
  Pallas kernels  103 us (45%)
  starting transfers between devices  43.2 us (19%)
  waiting for transfers between devices  42.2 us (19%)
  blocking collectives  33 us (14%)
  other arithmetic  3.36 us (1%)
    pallas_call x3, Pallas kernels, gram_sums(): pl.pallas_call(functools.partial(gram_body, spans=spans, parts=parts, pee...  87.4 us
    ppermute x17, starting transfers between devices, swap(): return lax.ppermute(block, axis, [(i, i ^ distance) for i in range(size)])  39.6 us
    all_to_all x1, blocking collectives, on_device(): lax.all_to_all(pieces[side], 'chan', split_axis=0, concat_axis=0, tiled=T...  33 us
    ppermute x17, waiting for transfers between devices, swap(): return lax.ppermute(block, axis, [(i, i ^ distance) for i in range(size)])  28.5 us
    all_to_all x1, waiting for transfers between devices, on_device(): lax.all_to_all(pieces[side], 'chan', split_axis=0, concat_axis=0, tiled=T...  13.8 us
    pallas_call x2, Pallas kernels, whitened(): pl.pallas_call(functools.partial(spectra_body, places=places), grid=(2,),...  10.1 us
    pallas_call x1, Pallas kernels, demodulate(): pl.pallas_call(demod_body, grid=(sensors // step,), in_specs=[pl.BlockSpe...  5.14 us
  transfers between devices with their start and end apart: 20, of which 8 were waited for; matrix products, arithmetic and copies ran while one was open for 1% of the time, Pallas kernels for 29%

profile of v3, /device:TPU:0, one launch (start us, length us, event | category | flops | bytes accessed | tf_op | source)
XLA Modules:
  0.0 226.5 jit_solution(7605850064519826697)
XLA Ops:
  0.0 5.1 %demod.1 = (f32[8,8,32,128]{3,2,1,0:T(8,128)}, f32[8,8,32,128]{3,2,1,0:T(8,128)}) custom-call(f32[2,32,64,128]{3,2,1,0:T(8,128)} %samples.1, bf16[128,256]{1,0:T(8,128)(2,1)} %constant.16.clone.table_high, bf16[128,256]{1,0:T(8,128)(2,1)} %constant.17.clone.table_low), custom_call_target="tpu_custom_call" | custom-call | tf_op jit(solution)/shard_map/demod/pallas_call | solution.py:82
  5.1 33.0 %all_to_all.10.received = f32[8,8,32,128]{3,2,1,0:T(8,128)} all-to-all(f32[8,8,32,128]{3,2,1,0:T(8,128)} %get-tuple-element.15), channel_id=1, replica_groups=mesh['sensor'=4,'chan'=8] {'chan'}, dimensions={0} | all-to-all | bytes 2097152 | tf_op jit(solution)/shard_map/all_to_all | solution.py:348
  38.2 3.6 %all-to-all-start = ((f32[8,8,32,128]{3,2,1,0:T(8,128)}), f32[8,8,32,128]{3,2,1,0:T(8,128)S(1)}, u32[]{:S(2)}, u32[]{:S(2)}) async-start(f32[8,8,32,128]{3,2,1,0:T(8,128)} %get-tuple-element.14), calls=%async_computation | async-start | bytes 2097152 | tf_op jit(solution)/shard_map/all_to_all | solution.py:348
  41.7 5.3 %spectra.3 = (f32[8,4,2,32,128]{4,3,2,1,0:T(8,128)}, f32[4,4,2,32,128]{4,3,2,1,0:T(8,128)}, f32[4,4,2,32,128]{4,3,2,1,0:T(8,128)}) custom-call(f32[8,8,32,128]{3,2,1,0:T(8,128)} %all_to_all.10.received, bf16[1024,512]{1,0:T(8,128)(2,1)} %constant.18.clone.table_high, bf16[1024,512]{1,0:T(8,128)(2,1)} %constant.19.clone.table_low), custom_call_target="tpu_custom_call" | custom-call | flops 1610612736 | bytes 8388608 | tf_op jit(solution)/shard_map/spectra/pallas_call | solution.py:133
  47.0 1.5 collective-permute-start.5
  48.5 1.5 collective-permute-start.8
  50.0 0.0 collective-permute-start.1
  50.0 0.5 collective-permute-start.7
  50.5 0.5 collective-permute-start.6
  51.1 11.0 %collective-permute-done.5.refs_6_ = f32[4,4,2,32,128]{4,3,2,1,0:T(8,128)S(1)} collective-permute-done((f32[4,4,2,32,128]{4,3,2,1,0:T(8,128)}, f32[4,4,2,32,128]{4,3,2,1,0:T(8,128)S(1)}, u32[]{:S(2)}, u32[]{:S(2)}) %collective-permute-start.5) | collective-permute-done | bytes 524320 | tf_op jit(solution)/shard_map/ppermute | solution.py:57
  62.0 0.0 copy-start.4
  62.0 1.5 collective-permute-start.9
  63.5 0.1 collective-permute-done.8.refs_9_
  63.6 1.4 collective-permute-start.10
  65.0 0.7 pad_add_fusion.ids
  65.7 13.8 %all-to-all-done.received = f32[8,8,32,128]{3,2,1,0:T(8,128)S(1)} async-done(((f32[8,8,32,128]{3,2,1,0:T(8,128)}), f32[8,8,32,128]{3,2,1,0:T(8,128)S(1)}, u32[]{:S(2)}, u32[]{:S(2)}) %all-to-all-start) | async-done | bytes 1048608 | tf_op jit(solution)/shard_map/all_to_all | solution.py:348
  79.5 0.0 copy-start
  79.5 1.0 copy-done
  80.4 4.8 %spectra.2.refs_1_.refs_2_.refs_3_ = f32[8,4,2,32,128]{4,3,2,1,0:T(8,128)} custom-call(f32[8,8,32,128]{3,2,1,0:T(8,128)} %copy-done, bf16[1024,512]{1,0:T(8,128)(2,1)} %constant.18.clone.table_high, bf16[1024,512]{1,0:T(8,128)(2,1)} %constant.19.clone.table_low), custom_call_target="tpu_custom_call" | custom-call | flops 1610612736 | bytes 8388608 | tf_op jit(solution)/shard_map/spectra/pallas_call | solution.py:133
  85.2 0.0 collective-permute-done.7.refs_8_
  85.2 2.4 %collective-permute-start.4 = (f32[8,4,2,32,128]{4,3,2,1,0:T(8,128)}, f32[8,4,2,32,128]{4,3,2,1,0:T(8,128)S(1)}, u32[]{:S(2)}, u32[]{:S(2)}) collective-permute-start(f32[8,4,2,32,128]{4,3,2,1,0:T(8,128)} %spectra.2.refs_1_.refs_2_.refs_3_), channel_id=1, source_target_pairs={{0,24},{8,16},{16,8},{24,0},{1,25},{9,17},{17,9},{25,1},{2,26},{10... | collective-permute-start | bytes 3145736 | tf_op jit(solution)/shard_map/ppermute | solution.py:57
  87.7 0.0 collective-permute-done.6.refs_7_
  87.7 0.5 collective-permute-start.3
  88.2 0.0 collective-permute-done.9.refs_10_
  88.2 0.5 collective-permute-start.2
  88.7 0.0 collective-permute-done.10.refs_11_
  88.7 0.0 collective-permute-start
  88.8 0.0 collective-permute-done.1.refs_0_.refs_1_
  88.8 0.0 copy-done.4
  88.8 0.0 copy-start.2
  88.8 1.0 copy-done.2
  89.7 40.4 %gram.3.refs_7_ = f32[64,2,32,128]{3,2,1,0:T(8,128)} custom-call(s32[2]{0:T(128)} %pad_add_fusion.ids, s32[64]{0:T(128)} %bins.5, s32[64]{0:T(128)} %offsets.5, f32[8,4,2,32,128]{4,3,2,1,0:T(8,128)} %copy-done.2, f32[8,4,2,32,128]{4,3,2,1,0:T(8,128)} %spectra.2.refs_1_.refs_2_.refs_3_, f32[4,4,2,32,128]{4,3,2,1,0:T(8,128)} %get-tuple-element.17.refs_2_.refs_4_, ...), custom_call_target="tpu_custom_call" | custom-call | flops 25769803776 | bytes 8388608 | tf_op jit(solution)/shard_map/gram/pallas_call | solution.py:309
  130.2 0.0 collective-permute-done.4.refs_6_
  130.2 0.0 copy-start.3
  130.2 3.4 %collective-permute-done.3.refs_5_ = f32[8,4,2,32,128]{4,3,2,1,0:T(8,128)} collective-permute-done((f32[8,4,2,32,128]{4,3,2,1,0:T(8,128)}, f32[8,4,2,32,128]{4,3,2,1,0:T(8,128)}, u32[]{:S(2)}, u32[]{:S(2)}) %collective-permute-start.3) | collective-permute-done | bytes 1048608 | tf_op jit(solution)/shard_map/ppermute | solution.py:57
  133.5 0.1 collective-permute-done.2.refs_4_
  133.6 0.0 collective-permute-done.refs_0_
  133.6 0.0 copy-done.3
  133.6 32.7 %gram.4 = (f32[24,2,32,128]{3,2,1,0:T(8,128)}, f32[24,2,32,128]{3,2,1,0:T(8,128)}) custom-call(s32[2]{0:T(128)} %pad_add_fusion.ids, s32[64]{0:T(128)} %bins.5, s32[64]{0:T(128)} %offsets.5, f32[8,4,2,32,128]{4,3,2,1,0:T(8,128)} %collective-permute-done.refs_0_, f32[8,4,2,32,128]{4,3,2,1,0:T(8,128)} %copy-done.2, ...), custom_call_target="tpu_custom_call" | custom-call | flops 19327352832 | bytes 8388608 | tf_op jit(solution)/shard_map/gram/pallas_call | solution.py:309
  166.3 0.0 copy-start.1
  166.4 20.0 %collective-permute-start.11 = (f32[24,2,32,128]{3,2,1,0:T(8,128)}, f32[24,2,32,128]{3,2,1,0:T(8,128)S(1)}, u32[]{:S(2)}, u32[]{:S(2)}) collective-permute-start(f32[24,2,32,128]{3,2,1,0:T(8,128)} %get-tuple-element.20), channel_id=1, source_target_pairs={{0,1},{1,0},{2,3},{3,2},{4,5},{5,4},{6,7},{7,6},{8,9},{9,8},{10,11... | collective-permute-start | bytes 2359304 | tf_op jit(solution)/shard_map/ppermute | solution.py:57
  186.4 14.3 %gram.5 = (f32[8,2,32,128]{3,2,1,0:T(8,128)}, f32[8,2,32,128]{3,2,1,0:T(8,128)}) custom-call(s32[2]{0:T(128)} %pad_add_fusion.ids, s32[64]{0:T(128)} %bins.5, s32[64]{0:T(128)} %offsets.5, f32[8,4,2,32,128]{4,3,2,1,0:T(8,128)} %collective-permute-done.refs_0_, f32[8,4,2,32,128]{4,3,2,1,0:T(8,128)} %copy-done.2, ...), custom_call_target="tpu_custom_call" | custom-call | flops 6442450944 | bytes 8388608 | tf_op jit(solution)/shard_map/gram/pallas_call | solution.py:309
  200.7 0.2 collective-permute-start.15
  200.9 1.6 collective-permute-done.15
  202.5 0.9 slice_add_fusion.6
  203.4 2.5 %collective-permute-start.17 = (f32[2,2,32,128]{3,2,1,0:T(8,128)S(1)}, f32[2,2,32,128]{3,2,1,0:T(8,128)S(1)}, u32[]{:S(2)}, u32[]{:S(2)}) collective-permute-start(f32[2,2,32,128]{3,2,1,0:T(8,128)S(1)} %get-tuple-element.26), channel_id=1, source_target_pairs={{0,4},{1,5},{2,6},{3,7},{4,0},{5,1},{6,2},{7,3},{8,12},{9,13},{10,... | collective-permute-start | bytes 196616 | tf_op jit(solution)/shard_map/ppermute | solution.py:57
  205.8 0.0 collective-permute-start.18
  205.9 1.9 collective-permute-start.16
  207.8 0.0 collective-permute-done.11
  207.9 0.0 copy-done.1
  207.9 0.1 slice_add_fusion.2
  208.0 1.6 collective-permute-start.13
  209.5 0.9 collective-permute-start.14
  210.5 0.0 collective-permute-done.17
  210.5 1.9 collective-permute-start.12
  212.4 0.0 collective-permute-done.18
  212.4 0.3 collective-permute-done.16
  212.7 0.9 fusion.1
  213.6 12.1 %collective-permute-done.13 = f32[6,2,32,128]{3,2,1,0:T(8,128)S(1)} collective-permute-done((f32[6,2,32,128]{3,2,1,0:T(8,128)S(1)}, f32[6,2,32,128]{3,2,1,0:T(8,128)S(1)}, u32[]{:S(2)}, u32[]{:S(2)}) %collective-permute-start.13) | collective-permute-done | bytes 196640 | tf_op jit(solution)/shard_map/ppermute | solution.py:57
  225.7 0.0 collective-permute-done.14
  225.7 0.0 collective-permute-done.12
  225.7 0.1 fusion
  225.8 0.7 pad_maximum_fusion
Async XLA Ops:
  38.2 41.3 %all-to-all-start = ((f32[8,8,32,128]{3,2,1,0:T(8,128)}), f32[8,8,32,128]{3,2,1,0:T(8,128)S(1)}, u32[]{:S(2)}, u32[]{:S(2)}) async-start(f32[8,8,32,128]{3,2,1,0:T(8,128)} %get-tuple-element.14), calls=%async_computation | async-start | bytes 2097152 | tf_op jit(solution)/shard_map/all_to_all | solution.py:348
  47.0 15.0 %collective-permute-start.5 = (f32[4,4,2,32,128]{4,3,2,1,0:T(8,128)}, f32[4,4,2,32,128]{4,3,2,1,0:T(8,128)S(1)}, u32[]{:S(2)}, u32[]{:S(2)}) collective-permute-start(f32[4,4,2,32,128]{4,3,2,1,0:T(8,128)} %get-tuple-element.17.refs_2_.refs_4_), channel_id=1, source_target_pairs={{0,8},{8,0},{16,24},{24,16},{1,9},{9,1},{17,25},{25,17},{2,10},{10... | collective-permute-start | bytes 1572872 | tf_op jit(solution)/shard_map/ppermute | solution.py:57
  48.5 15.1 %collective-permute-start.8 = (f32[4,4,2,32,128]{4,3,2,1,0:T(8,128)}, f32[4,4,2,32,128]{4,3,2,1,0:T(8,128)}, u32[]{:S(2)}, u32[]{:S(2)}) collective-permute-start(f32[4,4,2,32,128]{4,3,2,1,0:T(8,128)} %get-tuple-element.18.refs_3_.refs_5_), channel_id=1, source_target_pairs={{0,16},{8,24},{16,0},{24,8},{1,17},{9,25},{17,1},{25,9},{2,18},{10... | collective-permute-start | bytes 1572872 | tf_op jit(solution)/shard_map/ppermute | solution.py:57
  50.0 38.7 %collective-permute-start.1 = (f32[8,4,2,32,128]{4,3,2,1,0:T(8,128)}, f32[8,4,2,32,128]{4,3,2,1,0:T(8,128)S(1)}, u32[]{:S(2)}, u32[]{:S(2)}) collective-permute-start(f32[8,4,2,32,128]{4,3,2,1,0:T(8,128)} %get-tuple-element.16), channel_id=1, source_target_pairs={{0,1},{1,2},{2,3},{3,4},{4,5},{5,6},{6,7},{7,0},{8,9},{9,10},{10,1... | collective-permute-start | bytes 3145736 | tf_op jit(solution)/shard_map/ppermute | solution.py:351
  50.0 35.2 %collective-permute-start.7 = (f32[4,4,2,32,128]{4,3,2,1,0:T(8,128)}, f32[4,4,2,32,128]{4,3,2,1,0:T(8,128)}, u32[]{:S(2)}, u32[]{:S(2)}) collective-permute-start(f32[4,4,2,32,128]{4,3,2,1,0:T(8,128)} %get-tuple-element.17.refs_2_.refs_4_), channel_id=1, source_target_pairs={{0,16},{8,24},{16,0},{24,8},{1,17},{9,25},{17,1},{25,9},{2,18},{10... | collective-permute-start | bytes 1572872 | tf_op jit(solution)/shard_map/ppermute | solution.py:57
  50.5 37.2 %collective-permute-start.6 = (f32[4,4,2,32,128]{4,3,2,1,0:T(8,128)}, f32[4,4,2,32,128]{4,3,2,1,0:T(8,128)}, u32[]{:S(2)}, u32[]{:S(2)}) collective-permute-start(f32[4,4,2,32,128]{4,3,2,1,0:T(8,128)} %get-tuple-element.18.refs_3_.refs_5_), channel_id=1, source_target_pairs={{0,8},{8,0},{16,24},{24,16},{1,9},{9,1},{17,25},{25,17},{2,10},{10... | collective-permute-start | bytes 1572872 | tf_op jit(solution)/shard_map/ppermute | solution.py:57
  62.0 26.7 %copy-start.4 = (f32[4,4,2,32,128]{4,3,2,1,0:T(8,128)}, f32[4,4,2,32,128]{4,3,2,1,0:T(8,128)S(1)}, u32[]{:S(2)}) copy-start(f32[4,4,2,32,128]{4,3,2,1,0:T(8,128)S(1)} %collective-permute-done.5.refs_6_) | copy-start | bytes 1572868
  62.0 26.2 %collective-permute-start.9 = (f32[4,4,2,32,128]{4,3,2,1,0:T(8,128)S(1)}, f32[4,4,2,32,128]{4,3,2,1,0:T(8,128)}, u32[]{:S(2)}, u32[]{:S(2)}) collective-permute-start(f32[4,4,2,32,128]{4,3,2,1,0:T(8,128)S(1)} %collective-permute-done.5.refs_6_), channel_id=1, source_target_pairs={{0,16},{8,24},{16,0},{24,8},{1,17},{9,25},{17,1},{25,9},{2,18},{10... | collective-permute-start | bytes 1572872 | tf_op jit(solution)/shard_map/ppermute | solution.py:57
  63.6 25.1 %collective-permute-start.10 = (f32[4,4,2,32,128]{4,3,2,1,0:T(8,128)}, f32[4,4,2,32,128]{4,3,2,1,0:T(8,128)}, u32[]{:S(2)}, u32[]{:S(2)}) collective-permute-start(f32[4,4,2,32,128]{4,3,2,1,0:T(8,128)} %collective-permute-done.8.refs_9_), channel_id=1, source_target_pairs={{0,8},{8,0},{16,24},{24,16},{1,9},{9,1},{17,25},{25,17},{2,10},{10... | collective-permute-start | bytes 1572872 | tf_op jit(solution)/shard_map/ppermute | solution.py:57
  79.5 1.0 copy-start
  85.2 44.9 %collective-permute-start.4 = (f32[8,4,2,32,128]{4,3,2,1,0:T(8,128)}, f32[8,4,2,32,128]{4,3,2,1,0:T(8,128)S(1)}, u32[]{:S(2)}, u32[]{:S(2)}) collective-permute-start(f32[8,4,2,32,128]{4,3,2,1,0:T(8,128)} %spectra.2.refs_1_.refs_2_.refs_3_), channel_id=1, source_target_pairs={{0,24},{8,16},{16,8},{24,0},{1,25},{9,17},{17,9},{25,1},{2,26},{10... | collective-permute-start | bytes 3145736 | tf_op jit(solution)/shard_map/ppermute | solution.py:57
  87.7 45.8 %collective-permute-start.3 = (f32[8,4,2,32,128]{4,3,2,1,0:T(8,128)}, f32[8,4,2,32,128]{4,3,2,1,0:T(8,128)}, u32[]{:S(2)}, u32[]{:S(2)}) collective-permute-start(f32[8,4,2,32,128]{4,3,2,1,0:T(8,128)} %spectra.2.refs_1_.refs_2_.refs_3_), channel_id=1, source_target_pairs={{0,16},{8,24},{16,0},{24,8},{1,17},{9,25},{17,1},{25,9},{2,18},{10... | collective-permute-start | bytes 3145736 | tf_op jit(solution)/shard_map/ppermute | solution.py:57
  88.2 45.4 %collective-permute-start.2 = (f32[8,4,2,32,128]{4,3,2,1,0:T(8,128)}, f32[8,4,2,32,128]{4,3,2,1,0:T(8,128)}, u32[]{:S(2)}, u32[]{:S(2)}) collective-permute-start(f32[8,4,2,32,128]{4,3,2,1,0:T(8,128)} %spectra.2.refs_1_.refs_2_.refs_3_), channel_id=1, source_target_pairs={{0,8},{8,0},{16,24},{24,16},{1,9},{9,1},{17,25},{25,17},{2,10},{10... | collective-permute-start | bytes 3145736 | tf_op jit(solution)/shard_map/ppermute | solution.py:57
  88.7 44.9 %collective-permute-start = (f32[8,4,2,32,128]{4,3,2,1,0:T(8,128)}, f32[8,4,2,32,128]{4,3,2,1,0:T(8,128)}, u32[]{:S(2)}, u32[]{:S(2)}) collective-permute-start(f32[8,4,2,32,128]{4,3,2,1,0:T(8,128)} %spectra.2.refs_1_.refs_2_.refs_3_), channel_id=1, source_target_pairs={{0,1},{1,2},{2,3},{3,4},{4,5},{5,6},{6,7},{7,0},{8,9},{9,10},{10,1... | collective-permute-start | bytes 3145736 | tf_op jit(solution)/shard_map/ppermute | solution.py:366
  88.8 1.0 copy-start.2
  130.2 3.5 %copy-start.3 = (f32[8,4,2,32,128]{4,3,2,1,0:T(8,128)}, f32[8,4,2,32,128]{4,3,2,1,0:T(8,128)S(1)}, u32[]{:S(2)}) copy-start(f32[8,4,2,32,128]{4,3,2,1,0:T(8,128)S(1)} %collective-permute-done.4.refs_6_) | copy-start | bytes 3145732
  166.3 41.5 %copy-start.1 = (f32[24,2,32,128]{3,2,1,0:T(8,128)S(1)}, f32[24,2,32,128]{3,2,1,0:T(8,128)}, u32[]{:S(2)}) copy-start(f32[24,2,32,128]{3,2,1,0:T(8,128)} %get-tuple-element.19) | copy-start | bytes 2359300
  166.4 41.5 %collective-permute-start.11 = (f32[24,2,32,128]{3,2,1,0:T(8,128)}, f32[24,2,32,128]{3,2,1,0:T(8,128)S(1)}, u32[]{:S(2)}, u32[]{:S(2)}) collective-permute-start(f32[24,2,32,128]{3,2,1,0:T(8,128)} %get-tuple-element.20), channel_id=1, source_target_pairs={{0,1},{1,0},{2,3},{3,2},{4,5},{5,4},{6,7},{7,6},{8,9},{9,8},{10,11... | collective-permute-start | bytes 2359304 | tf_op jit(solution)/shard_map/ppermute | solution.py:57
  200.7 1.8 collective-permute-start.15
  203.4 7.1 %collective-permute-start.17 = (f32[2,2,32,128]{3,2,1,0:T(8,128)S(1)}, f32[2,2,32,128]{3,2,1,0:T(8,128)S(1)}, u32[]{:S(2)}, u32[]{:S(2)}) collective-permute-start(f32[2,2,32,128]{3,2,1,0:T(8,128)S(1)} %get-tuple-element.26), channel_id=1, source_target_pairs={{0,4},{1,5},{2,6},{3,7},{4,0},{5,1},{6,2},{7,3},{8,12},{9,13},{10,... | collective-permute-start | bytes 196616 | tf_op jit(solution)/shard_map/ppermute | solution.py:57
  205.8 6.6 %collective-permute-start.18 = (f32[2,2,32,128]{3,2,1,0:T(8,128)S(1)}, f32[2,2,32,128]{3,2,1,0:T(8,128)S(1)}, u32[]{:S(2)}, u32[]{:S(2)}) collective-permute-start(f32[2,2,32,128]{3,2,1,0:T(8,128)S(1)} %get-tuple-element.27), channel_id=1, source_target_pairs={{0,2},{1,3},{2,0},{3,1},{4,6},{5,7},{6,4},{7,5},{8,10},{9,11},{10,... | collective-permute-start | bytes 196616 | tf_op jit(solution)/shard_map/ppermute | solution.py:57
  205.9 6.8 %collective-permute-start.16 = (f32[2,2,32,128]{3,2,1,0:T(8,128)S(1)}, f32[2,2,32,128]{3,2,1,0:T(8,128)S(1)}, u32[]{:S(2)}, u32[]{:S(2)}) collective-permute-start(f32[2,2,32,128]{3,2,1,0:T(8,128)S(1)} %get-tuple-element.28), channel_id=1, source_target_pairs={{0,6},{1,7},{2,4},{3,5},{4,2},{5,3},{6,0},{7,1},{8,14},{9,15},{10,... | collective-permute-start | bytes 196616 | tf_op jit(solution)/shard_map/ppermute | solution.py:57
  208.0 17.7 %collective-permute-start.13 = (f32[6,2,32,128]{3,2,1,0:T(8,128)S(1)}, f32[6,2,32,128]{3,2,1,0:T(8,128)S(1)}, u32[]{:S(2)}, u32[]{:S(2)}) collective-permute-start(f32[6,2,32,128]{3,2,1,0:T(8,128)S(1)} %get-tuple-element.23), channel_id=1, source_target_pairs={{0,4},{1,5},{2,6},{3,7},{4,0},{5,1},{6,2},{7,3},{8,12},{9,13},{10,... | collective-permute-start | bytes 589832 | tf_op jit(solution)/shard_map/ppermute | solution.py:57
  209.5 16.1 %collective-permute-start.14 = (f32[6,2,32,128]{3,2,1,0:T(8,128)S(1)}, f32[6,2,32,128]{3,2,1,0:T(8,128)S(1)}, u32[]{:S(2)}, u32[]{:S(2)}) collective-permute-start(f32[6,2,32,128]{3,2,1,0:T(8,128)S(1)} %get-tuple-element.24), channel_id=1, source_target_pairs={{0,2},{1,3},{2,0},{3,1},{4,6},{5,7},{6,4},{7,5},{8,10},{9,11},{10,... | collective-permute-start | bytes 589832 | tf_op jit(solution)/shard_map/ppermute | solution.py:57
  210.5 15.2 %collective-permute-start.12 = (f32[6,2,32,128]{3,2,1,0:T(8,128)S(1)}, f32[6,2,32,128]{3,2,1,0:T(8,128)S(1)}, u32[]{:S(2)}, u32[]{:S(2)}) collective-permute-start(f32[6,2,32,128]{3,2,1,0:T(8,128)S(1)} %get-tuple-element.25), channel_id=1, source_target_pairs={{0,6},{1,7},{2,4},{3,5},{4,2},{5,3},{6,0},{7,1},{8,14},{9,15},{10,... | collective-permute-start | bytes 589832 | tf_op jit(solution)/shard_map/ppermute | solution.py:57
